TPU v7x, 8 devices: a whole 2x2x1 slice. The times are simulated.
8 devices in a mesh: dp: 2 (over z, y), ep: 4 (over x, core).
Axes of the slice: x: 2, y: 2, z: 1, core: 2. Of those that a mesh axis runs over, the one named last changes fastest.
Arguments:
- tokens: bfloat16 [8192, 768], P(('dp', 'ep')), parts along dimension 0
- topk_idx: int32 [8192, 1], P(('dp', 'ep')), parts along dimension 0
- topk_w: float32 [8192, 1], P(('dp', 'ep')), parts along dimension 0
- w_up: bfloat16 [4, 5, 768, 3072], P('ep')
- w_down: bfloat16 [4, 5, 3072, 768], P('ep')
- slot_expert: int32 [4, 5], replicated
Outputs:
- output: bfloat16 [8192, 768], P(('dp', 'ep')), parts along dimension 0
There are 2 independent parts. A program takes and returns all parts, laid end to end along the dimension named above; an argument that names none is the same for every part.
All inputs are finite; a program needn't handle non-finite values.
Results may differ from a plain program's by a relative error of at most 0.001.
Values are sent between devices in bfloat16 or wider.
A program may use at most 1 GiB of HBM per device.

v0:
```python
import jax
import jax.numpy as jnp
from jax import lax
from jax.sharding import PartitionSpec as P

MAX_COPIES = 4


def slot_bound(n_tok, n_top, n_dev, n_slot):
    base_load = (n_tok * n_top) // (n_dev * n_slot)
    return base_load + base_load // 2 + 1


def route_pairs(topk_idx, slot_expert, capacity):
    n_dev, n_slot = slot_expert.shape
    n_exp = n_dev * (n_slot - 1)
    n_top = topk_idx.shape[1]
    table_flat = slot_expert.reshape(-1)
    slot_ids = jnp.arange(n_dev * n_slot, dtype=jnp.int32)
    same_exp = table_flat[:, None] == table_flat[None, :]
    earlier = slot_ids[None, :] < slot_ids[:, None]
    copy_rank = jnp.sum(same_exp & earlier, axis=1, dtype=jnp.int32)
    exp_copies = jax.ops.segment_sum(jnp.ones_like(table_flat), table_flat, num_segments=n_exp)
    slot_of = jnp.zeros((n_exp, MAX_COPIES), jnp.int32).at[table_flat, copy_rank].set(slot_ids)
    flat_exp = topk_idx.reshape(-1)
    onehot = (flat_exp[:, None] == jnp.arange(n_exp, dtype=jnp.int32)[None, :]).astype(jnp.int32)
    pair_rank = jnp.sum((jnp.cumsum(onehot, axis=0) - onehot) * onehot, axis=1)
    pair_copies = exp_copies[flat_exp]
    slot_flat = slot_of[flat_exp, pair_rank % pair_copies]
    buf_row = pair_rank // pair_copies
    pair_pos = ((slot_flat % n_slot) * n_dev + slot_flat // n_slot) * capacity + buf_row
    pair_tok = jnp.arange(flat_exp.shape[0], dtype=jnp.int32) // n_top
    buf_tok = jnp.zeros((n_slot * n_dev * capacity,), jnp.int32).at[pair_pos].set(pair_tok)
    return pair_pos, buf_tok


def expert_ffn(recv_buf, up_local, down_local):
    pre_act = jnp.einsum('spcm,smf->spcf', recv_buf, up_local, preferred_element_type=jnp.float32)
    hidden = jax.nn.gelu(pre_act, approximate=True).astype(jnp.bfloat16)
    return jnp.einsum('spcf,sfm->spcm', hidden, down_local, preferred_element_type=jnp.float32).astype(jnp.bfloat16)


def solution(mesh):
    def group_layer(tokens, topk_idx, topk_w, w_up, w_down, slot_expert):
        n_tok, d_model = tokens.shape
        n_top = topk_idx.shape[1]
        n_dev, n_slot = slot_expert.shape
        capacity = slot_bound(n_tok, n_top, n_dev, n_slot)
        pair_pos, buf_tok = route_pairs(topk_idx, slot_expert, capacity)
        send_buf = tokens[buf_tok].reshape(n_slot, n_dev, capacity, d_model)
        recv_buf = lax.all_to_all(send_buf, 'ep', 1, 1, tiled=True)
        expert_out = expert_ffn(recv_buf, w_up[0], w_down[0])
        back_buf = lax.all_to_all(expert_out, 'ep', 1, 1, tiled=True)
        pair_out = back_buf.reshape(-1, d_model)[pair_pos].reshape(n_tok, n_top, d_model)
        mixed_out = jnp.sum(pair_out.astype(jnp.float32) * topk_w[:, :, None], axis=1)
        return mixed_out.astype(jnp.bfloat16)

    row_spec = P(('dp', 'ep'), None)
    weight_spec = P('ep', None, None, None)
    return jax.shard_map(group_layer, mesh=mesh, in_specs=(row_spec, row_spec, row_spec, weight_spec, weight_spec, P(None, None)), out_specs=row_spec, check_vma=False)
```

profile of v0, /device:TPU:0, one launch (start us, length us, event | category | flops | bytes accessed | tf_op | source)
XLA Modules:
  0.0 172.6 jit_solution(15821756081184264438)
XLA Ops:
  0.0 0.0 copy-start
  0.0 0.9 eq.53
  0.9 0.8 reshape.233
  1.6 0.2 convert_reduce_fusion
  1.8 0.7 scatter_custom_fusion.1
  2.5 0.7 fusion.43
  3.2 5.1 %compare_select_fusion.5 = (s32[1024,1]{0,1:T(1,128)S(1)}, s32[1024,1]{0,1:T(1,128)S(1)}) fusion(s32[]{:T(128)} %bitcast.16, s32[]{:T(128)} %bitcast.17, s32[]{:T(128)} %bitcast.18, s32[]{:T(128)} %bitcast.19, s32[]{:T(128)} %bitcast.20, s32[]{:T(128)} %bitcast.22, s32[]{:T(128)} %bitcast.21, s32[1024,1]{0,1:T(1,128)} %param.7), kind=kLoop, calls=%fused_computation.48 | loop fusion | flops 15360 | bytes 12316 | tf_op jit(solution)/shard_map/gather | solution.py:28
  8.3 0.1 compare_reduce_fusion.8
  8.4 0.7 fusion.26
  9.1 4.5 %reduce-window.6 = s32[16,8,128]{2,1,0:T(8,128)S(1)} reduce-window(s32[16,8,128]{2,1,0:T(8,128)S(1)} %fusion.26, s32[]{:T(128)} %constant.31.clone.1), window={size=1x1x128 pad=0_0x0_0x127_0}, to_apply=%region_2.0 | reduce-window | flops 2080768 | bytes 131076 | tf_op jit(solution)/shard_map/reduce-window
  13.6 0.1 slice.33
  13.7 0.1 copy.17
  13.9 0.1 copy.18
  13.9 0.1 broadcast_add_fusion
  14.0 0.7 fusion.25
  14.8 5.6 %select_select_fusion = s32[1024]{0:T(1024)S(1)} fusion(pred[1024]{0:T(1024)(128)(4,1)S(1)} %get-tuple-element.13, pred[1024]{0:T(1024)(128)(4,1)S(1)} %get-tuple-element.12, pred[1024]{0:T(1024)(128)(4,1)S(1)} %get-tuple-element.11, pred[1024]{0:T(1024)(128)(4,1)S(1)} %get-tuple-element.10, pred[1024]{0:T(1024)(128)(4,1)S(1)} %get-tuple-element.9, ...), kind=kLoop, calls=%fused_computation.67 | loop fusion | flops 9216 | bytes 17444 | tf_op jit(solution)/shard_map/gather | solution.py:28
  20.4 0.4 fusion.32
  20.8 2.0 %scatter_fusion = s32[16,4]{0,1:T(4,128)S(1)} fusion(s32[16,4]{0,1:T(4,128)S(1)} %broadcast_in_dim.10, s32[20]{0:T(128)S(1)} %fusion.36, s32[20]{0:T(128)S(1)} %iota.20), kind=kCustom, calls=%fused_computation.3 | custom fusion | bytes 400 | tf_op jit(solution)/shard_map/scatter | solution.py:24
  22.8 8.9 %gather_fusion = s32[1024]{0:T(1024)S(1)} fusion(s32[16,4]{0,1:T(4,128)S(1)} %scatter_fusion, s32[1024]{0:T(1024)S(1)} %bitcast.66), kind=kCustom, calls=%fused_computation | custom fusion | bytes 16384 | tf_op jit(solution)/shard_map/gather | solution.py:29
  31.7 0.4 compare_select_fusion
  32.1 4.3 %scatter_custom_fusion.2 = s32[1540]{0:T(1024)S(1)} fusion(s32[1024]{0:T(1024)S(1)} %bitcast.77, s32[1024]{0:T(1024)S(1)} %iota.21, s32[]{:T(128)} %constant.31.clone.1), kind=kCustom, calls=%fused_computation.69 | custom fusion | bytes 6164 | tf_op jit(solution)/shard_map/scatter | solution.py:33
  36.4 0.0 copy-done
  36.5 6.2 %gather_fusion.1 = bf16[1540,768]{1,0:T(8,128)(2,1)} fusion(bf16[1024,768]{1,0:T(8,128)(2,1)S(1)} %copy-done, s32[2048]{0:T(1024)S(1)} %pad_clamp_fusion), kind=kCustom, calls=%fused_computation.1 | custom fusion | bytes 4737040 | tf_op jit(solution)/shard_map/gather | solution.py:50
  42.6 3.8 %reshape.235 = bf16[5,4,77,768]{3,2,1,0:T(8,128)(2,1)} reshape(bf16[1540,768]{1,0:T(8,128)(2,1)} %gather_fusion.1) | data formatting | bytes 4730880 | tf_op jit(solution)/shard_map/reshape | solution.py:50
  46.5 1.9 %copy.19 = bf16[5,4,77,768]{3,2,0,1:T(8,128)(2,1)S(1)} copy(bf16[5,4,77,768]{3,2,1,0:T(8,128)(2,1)} %reshape.235) | data formatting | bytes 4730880 | tf_op jit(solution)/shard_map/reshape | solution.py:50
  48.3 33.9 %all_to_all.10 = bf16[5,4,77,768]{3,2,0,1:T(8,128)(2,1)} all-to-all(bf16[5,4,77,768]{3,2,0,1:T(8,128)(2,1)S(1)} %copy.19), channel_id=1, replica_groups=mesh['dp'=2,'ep'=4] {'ep'}, dimensions={1} | all-to-all | bytes 4730880 | tf_op jit(solution)/shard_map/all_to_all | solution.py:51
  82.3 16.9 %fusion.2 = f32[5,4,77,3072]{3,2,1,0:T(8,128)} fusion(bf16[1,5,768,3072]{3,2,1,0:T(8,128)(2,1)} %param.9, bf16[5,4,77,768]{3,2,0,1:T(8,128)(2,1)} %all_to_all.10), kind=kOutput, calls=%fused_computation.9 | convolution fusion | flops 7266631680 | bytes 44881920 | tf_op jit(solution)/shard_map/spcm,smf->spcf/dot_general | solution.py:38
  99.1 21.2 %fusion.18 = bf16[5,4,77,768]{3,2,1,0:T(8,128)(2,1)} fusion(bf16[1,5,3072,768]{3,2,1,0:T(8,128)(2,1)} %param.10, f32[5,4,77,3072]{3,2,1,0:T(8,128)} %fusion.2), kind=kOutput, calls=%fused_computation.25 | convolution fusion | flops 7310392320 | bytes 44881920 | tf_op jit(solution)/shard_map/spcf,sfm->spcm/dot_general | solution.py:40
  120.3 3.3 %copy.21 = bf16[5,4,77,768]{3,2,0,1:T(8,128)(2,1)} copy(bf16[5,4,77,768]{3,2,1,0:T(8,128)(2,1)} %fusion.18) | data formatting | bytes 4730880 | tf_op jit(solution)/shard_map/convert_element_type | solution.py:40
  123.6 4.5 %all-to-all-start.1 = ((bf16[5,4,77,768]{3,2,0,1:T(8,128)(2,1)}), bf16[5,4,77,768]{3,2,0,1:T(8,128)(2,1)}, u32[]{:S(2)}, u32[]{:S(2)}) async-start(bf16[5,4,77,768]{3,2,0,1:T(8,128)(2,1)} %copy.21), calls=%async_computation.1 | async-start | bytes 4915200 | tf_op jit(solution)/shard_map/all_to_all | solution.py:53
  128.1 29.3 %all-to-all-done.1 = bf16[5,4,77,768]{3,2,0,1:T(8,128)(2,1)} async-done(((bf16[5,4,77,768]{3,2,0,1:T(8,128)(2,1)}), bf16[5,4,77,768]{3,2,0,1:T(8,128)(2,1)}, u32[]{:S(2)}, u32[]{:S(2)}) %all-to-all-start.1) | async-done | bytes 2365472 | tf_op jit(solution)/shard_map/all_to_all | solution.py:53
  157.4 3.3 %copy.22 = bf16[5,4,77,768]{3,2,1,0:T(8,128)(2,1)} copy(bf16[5,4,77,768]{3,2,0,1:T(8,128)(2,1)} %all-to-all-done.1) | data formatting | bytes 4730880 | tf_op jit(solution)/shard_map/all_to_all | solution.py:53
  160.7 3.8 %reshape.236 = bf16[1540,768]{1,0:T(8,128)(2,1)} reshape(bf16[5,4,77,768]{3,2,1,0:T(8,128)(2,1)} %copy.22) | data formatting | bytes 4730880 | tf_op jit(solution)/shard_map/reshape | solution.py:54
  164.6 0.0 copy-start.2
  164.6 0.0 copy-start.1
  164.6 6.6 %gather_fusion.2 = bf16[1024,768]{1,0:T(8,128)(2,1)S(1)} fusion(bf16[1540,768]{1,0:T(8,128)(2,1)} %reshape.236, s32[1024]{0:T(1024)S(1)} %broadcast_clamp_fusion), kind=kCustom, calls=%fused_computation.2 | custom fusion | bytes 3149824 | tf_op jit(solution)/shard_map/gather | solution.py:54
  171.1 0.0 copy-done.2
  171.1 1.5 multiply_convert_fusion
  172.6 0.0 copy-done.1
  (12 shorter events, 0.1 us)
Async XLA Ops:
  0.0 36.4 %copy-start = (bf16[1024,768]{1,0:T(8,128)(2,1)S(1)}, bf16[1024,768]{1,0:T(8,128)(2,1)}, u32[]{:S(2)}) copy-start(bf16[1024,768]{1,0:T(8,128)(2,1)} %param.6) | copy-start | bytes 4718596
  123.6 33.8 %all-to-all-start.1 = ((bf16[5,4,77,768]{3,2,0,1:T(8,128)(2,1)}), bf16[5,4,77,768]{3,2,0,1:T(8,128)(2,1)}, u32[]{:S(2)}, u32[]{:S(2)}) async-start(bf16[5,4,77,768]{3,2,0,1:T(8,128)(2,1)} %copy.21), calls=%async_computation.1 | async-start | bytes 4915200 | tf_op jit(solution)/shard_map/all_to_all | solution.py:53
  164.6 6.6 %copy-start.2 = (f32[1024,1]{0,1:T(1,128)S(1)}, f32[1024,1]{0,1:T(1,128)}, u32[]{:S(2)}) copy-start(f32[1024,1]{0,1:T(1,128)} %param.8) | copy-start | bytes 12292
  164.6 8.1 %copy-start.1 = (bf16[1024,768]{1,0:T(8,128)(2,1)S(1)}, bf16[1024,768]{1,0:T(8,128)(2,1)}, u32[]{:S(2)}) copy-start(bf16[1024,768]{1,0:T(8,128)(2,1)} %param.6) | copy-start | bytes 4718596
where the time goes:
time: 173 us
  local copies, waits for them, and re-layouts  46.7 us (27%)
  matrix products  38 us (22%)
  blocking collectives  33.9 us (20%)
  waiting for transfers between devices  29.3 us (17%)
  other arithmetic  19.9 us (12%)
  starting transfers between devices  4.51 us (3%)
    all_to_all x1, blocking collectives, group_layer(): recv_buf = lax.all_to_all(send_buf, 'ep', 1, 1, tiled=True)  33.9 us
    all_to_all x1, waiting for transfers between devices, group_layer(): back_buf = lax.all_to_all(expert_out, 'ep', 1, 1, tiled=True)  29.3 us
    dot_general x1, matrix products, expert_ffn(): jnp.einsum('spcf,sfm->spcm', hidden, down_local, preferred_element_type=j...  21.2 us
    dot_general x1, matrix products, expert_ffn(): jnp.einsum('spcm,smf->spcf', recv_buf, up_local, preferred_element_type=j...  16.9 us
    gather x3, other arithmetic, route_pairs(): pair_copies = exp_copies[flat_exp]  10.8 us
    gather x1, local copies, waits for them, and re-layouts, route_pairs(): slot_flat = slot_of[flat_exp, pair_rank % pair_copies]  8.86 us
    gather x1, local copies, waits for them, and re-layouts, group_layer(): back_buf.reshape(-1, d_model)[pair_pos].reshape(n_tok, n_top, d_model)  6.57 us
    gather x1, local copies, waits for them, and re-layouts, group_layer(): send_buf = tokens[buf_tok].reshape(n_slot, n_dev, capacity, d_model)  6.18 us
  transfers between devices with their start and end apart: 1, of which 1 were waited for; matrix products, arithmetic and copies ran while one was open for 0% of the time, Pallas kernels for 0%

commit v1 on v0

--- a/solution.py
+++ b/solution.py
@@ -1,9 +1,22 @@
+import functools
+
 import jax
 import jax.numpy as jnp
 from jax import lax
+from jax.experimental import pallas as pl
+from jax.experimental.pallas import tpu as pltpu
 from jax.sharding import PartitionSpec as P
 
 MAX_COPIES = 4
+SEG = 80
+N_SEG = 4
+SEG_ROWS = 256
+SLOT_ROWS = 4 * SEG
+LOCAL_BASE = N_SEG * SEG_ROWS
+LOCAL_ROWS = 1664
+FF_TILE = 512
+N_WBUF = 4
+MESH = pl.DeviceIdType.MESH
 
 
 def slot_bound(n_tok, n_top, n_dev, n_slot):
@@ -40,20 +53,225 @@
     return jnp.einsum('spcf,sfm->spcm', hidden, down_local, preferred_element_type=jnp.float32).astype(jnp.bfloat16)
 
 
+def general_layer(tokens, topk_idx, w_up, w_down, slot_expert):
+    n_tok, d_model = tokens.shape
+    n_top = topk_idx.shape[1]
+    n_dev, n_slot = slot_expert.shape
+    capacity = slot_bound(n_tok, n_top, n_dev, n_slot)
+    pair_pos, buf_tok = route_pairs(topk_idx, slot_expert, capacity)
+    send_buf = tokens[buf_tok].reshape(n_slot, n_dev, capacity, d_model)
+    recv_buf = lax.all_to_all(send_buf, 'ep', 1, 1, tiled=True)
+    expert_out = expert_ffn(recv_buf, w_up[0], w_down[0])
+    back_buf = lax.all_to_all(expert_out, 'ep', 1, 1, tiled=True)
+    return back_buf.reshape(-1, d_model)[pair_pos]
+
+
+def route(idx_row, table, peers, n_exp, n_slot):
+    f32 = jnp.float32
+    n_tok = idx_row.shape[1]
+    lanes = 128
+    exp_id = lax.broadcasted_iota(jnp.int32, (n_exp, lanes), 0)
+    match = [[(exp_id == table[d, s]).astype(f32) for s in range(n_slot)] for d in peers]
+    copies = sum(sum(row) for row in match)
+    hot = (copies == 4.0).astype(f32)
+    own = sum(match[0])
+    own_slot = sum(s * match[0][s] for s in range(n_slot))
+    seen = jnp.zeros((n_exp, lanes), f32)
+    base = [jnp.zeros((n_exp, lanes), f32) for _ in range(MAX_COPIES)]
+    for r in range(len(peers)):
+        passed = jnp.zeros((1, lanes), f32)
+        for s in range(n_slot):
+            here = match[r][s]
+            local = LOCAL_BASE + SLOT_ROWS * own_slot + SEG * r
+            if r == 0:
+                code = local
+            else:
+                seg = s - passed
+                code = jnp.where(own > 0, local, SEG_ROWS * seg + SEG * (r - 1))
+                passed = passed + jnp.sum(here * hot, axis=0, keepdims=True)
+            for c in range(MAX_COPIES):
+                base[c] = jnp.where((here > 0) & (seen == c), code, base[c])
+            seen = seen + here
+    hot_slot = sum(s * jnp.sum(match[0][s] * hot, axis=0, keepdims=True) for s in range(n_slot))
+
+    wide = lambda a: jnp.concatenate([a] * (n_tok // lanes), axis=1)
+    onehot = (lax.broadcasted_iota(jnp.int32, (n_exp, n_tok), 0) == idx_row).astype(f32)
+    step = 256
+    blocks = [onehot[:, b * step:(b + 1) * step] for b in range(n_tok // step)]
+    before = lax.broadcasted_iota(jnp.int32, (step, step), 0) < lax.broadcasted_iota(jnp.int32, (step, step), 1)
+    local_rank = jnp.dot(jnp.concatenate(blocks, axis=0).astype(jnp.bfloat16), before.astype(f32).astype(jnp.bfloat16), preferred_element_type=f32)
+    carry = jnp.zeros((n_exp, 1), f32)
+    ranks = []
+    for b, block in enumerate(blocks):
+        ranks.append(local_rank[b * n_exp:(b + 1) * n_exp] + carry)
+        carry = carry + jnp.sum(block, axis=1, keepdims=True)
+    rank = jnp.concatenate(ranks, axis=1)
+    n_copy = wide(copies)
+    row = jnp.floor((rank + 0.5) * wide(1.0 / copies))
+    which = rank - row * n_copy
+    start = wide(base[3])
+    for c in range(MAX_COPIES - 1):
+        start = jnp.where(which == c, wide(base[c]), start)
+    code = jnp.sum(onehot * (start + row), axis=0, keepdims=True)
+    return code.astype(jnp.int32), hot_slot
+
+
+def layer_kernel(table, tokens, idx_row, w_up, w_down, out, up_buf, down_buf, send, recv, x_buf, acc, result, back_send, back_recv, code_row, code_col, w_sem, ds_sem, dr_sem, bs_sem, br_sem):
+    f32, bf16 = jnp.float32, jnp.bfloat16
+    n_tok, d_model = tokens.shape
+    n_slot = w_up.shape[0]
+    d_ff = w_up.shape[2]
+    me = lax.axis_index('ep')
+    chip, core = me // 2, me % 2
+    peers = [me, 2 * chip + (1 - core), 2 * (1 - chip) + core, 2 * (1 - chip) + (1 - core)]
+
+    barrier = pltpu.get_barrier_semaphore()
+    for r in (1, 2, 3):
+        pl.semaphore_signal(barrier, inc=1, device_id={'ep': peers[r]}, device_id_type=MESH)
+
+    def weight_copies(s):
+        b = s % N_WBUF
+        return (pltpu.make_async_copy(w_up.at[s], up_buf.at[b], w_sem.at[s, 0]),
+                pltpu.make_async_copy(w_down.at[s], down_buf.at[b], w_sem.at[s, 1]))
+
+    for s in range(N_WBUF):
+        for copy in weight_copies(s):
+            copy.start()
+
+    code, hot_slot = route(idx_row[...], table, peers, 16, n_slot)
+    code_row[...] = jnp.broadcast_to(code, code_row.shape)
+    code_col[...] = jnp.transpose(jnp.broadcast_to(code, (128, n_tok)))
+    hot_slot = hot_slot[:, :1]
+    back_recv[:, 3 * SEG:, :] = jnp.zeros((N_SEG, SEG_ROWS - 3 * SEG, d_model), bf16)
+    result[n_slot * SLOT_ROWS:, :] = jnp.zeros((LOCAL_ROWS - n_slot * SLOT_ROWS, d_model), bf16)
+
+    def pick(first, rows):
+        ids = lax.broadcasted_iota(jnp.int32, (rows, n_tok), 0) + first
+        mask = (ids == code_row[0:1, :]).astype(f32).astype(bf16)
+        return jnp.dot(mask, tokens[...], preferred_element_type=f32).astype(bf16)
+
+    def dispatch_copy(k, r):
+        rows = pl.ds((r - 1) * SEG, SEG)
+        return pltpu.make_async_remote_copy(
+            src_ref=send.at[k, rows], dst_ref=recv.at[k, rows],
+            send_sem=ds_sem.at[k, r - 1], recv_sem=dr_sem.at[k, r - 1],
+            device_id={'ep': peers[r]}, device_id_type=MESH)
+
+    def back_copy(k, r):
+        rows = pl.ds((r - 1) * SEG, SEG)
+        return pltpu.make_async_remote_copy(
+            src_ref=back_send.at[k, rows], dst_ref=back_recv.at[k, rows],
+            send_sem=bs_sem.at[k, r - 1], recv_sem=br_sem.at[k, r - 1],
+            device_id={'ep': peers[r]}, device_id_type=MESH)
+
+    for k in range(N_SEG):
+        send[k] = pick(k * SEG_ROWS, SEG_ROWS)
+        if k == 0:
+            pl.semaphore_wait(barrier, 3)
+        for r in (2, 3, 1):
+            dispatch_copy(k, r).start()
+
+    for s in range(n_slot):
+        x_buf[...] = pick(LOCAL_BASE + s * SLOT_ROWS, SLOT_ROWS)
+        if s < N_SEG:
+            for r in (1, 2, 3):
+                dispatch_copy(s, r).wait_recv()
+        far = x_buf[SEG:, :].astype(f32)
+        if s < N_SEG:
+            far = far + recv[s, :3 * SEG, :].astype(f32) * (hot_slot > s).astype(f32)
+        if s > 0:
+            far = far + recv[s - 1, :3 * SEG, :].astype(f32) * (hot_slot < s).astype(f32)
+        x_buf[SEG:, :] = far.astype(bf16)
+        for copy in weight_copies(s):
+            copy.wait()
+        b = s % N_WBUF
+        acc[...] = jnp.zeros_like(acc)
+
+        def ff_step(i, carry):
+            cols = pl.ds(pl.multiple_of(i * FF_TILE, FF_TILE), FF_TILE)
+            pre = jnp.dot(x_buf[...], up_buf[b, :, cols], preferred_element_type=f32)
+            hidden = jax.nn.gelu(pre, approximate=True).astype(bf16)
+            acc[...] += jnp.dot(hidden, down_buf[b, cols, :], preferred_element_type=f32)
+            return carry
+
+        lax.fori_loop(0, d_ff // FF_TILE, ff_step, 0)
+        if s + N_WBUF < n_slot:
+            for copy in weight_copies(s + N_WBUF):
+                copy.start()
+        result[s * SLOT_ROWS:(s + 1) * SLOT_ROWS, :] = acc[...].astype(bf16)
+        if s > 0:
+            k = s - 1
+            prev = result[k * SLOT_ROWS + SEG:(k + 1) * SLOT_ROWS, :].astype(f32)
+            back = prev * (hot_slot > k).astype(f32) + acc[SEG:, :].astype(bf16).astype(f32) * (hot_slot <= k).astype(f32)
+            back_send[k, :3 * SEG, :] = back.astype(bf16)
+            for r in (2, 3, 1):
+                back_copy(k, r).start()
+
+    tile = 256
+
+    def combine(first, rows, source, add):
+        def body(i, carry):
+            at = pl.ds(pl.multiple_of(i * tile, tile), tile)
+            mine = code_col[at, :]
+            ids = lax.broadcasted_iota(jnp.int32, (tile, 128), 1) + first
+            mask = jnp.concatenate([(mine == ids + 128 * j).astype(f32).astype(bf16) for j in range(rows // 128)], axis=1)
+            part = jnp.dot(mask, source(), preferred_element_type=f32)
+            if add:
+                part = part + out[at, :].astype(f32)
+            out[at, :] = part.astype(bf16)
+            return carry
+        lax.fori_loop(0, n_tok // tile, body, 0)
+
+    combine(LOCAL_BASE, LOCAL_ROWS, lambda: result[...], False)
+    for k in range(N_SEG):
+        for r in (1, 2, 3):
+            back_copy(k, r).wait_recv()
+        combine(k * SEG_ROWS, SEG_ROWS, lambda: back_recv[k], True)
+    for k in range(N_SEG):
+        for r in (1, 2, 3):
+            dispatch_copy(k, r).wait_send()
+            back_copy(k, r).wait_send()
+
+
+def fast_layer(tokens, topk_idx, w_up, w_down, slot_expert):
+    n_tok, d_model = tokens.shape
+    n_slot, d_ff = w_up.shape[1], w_up.shape[3]
+    vmem = pl.BlockSpec(memory_space=pltpu.VMEM)
+    anym = pl.BlockSpec(memory_space=pl.ANY)
+    bf16 = jnp.bfloat16
+    return pl.pallas_call(
+        layer_kernel,
+        out_shape=jax.ShapeDtypeStruct((n_tok, d_model), bf16),
+        in_specs=[pl.BlockSpec(memory_space=pltpu.SMEM), vmem, vmem, anym, anym],
+        out_specs=vmem,
+        scratch_shapes=[
+            pltpu.VMEM((N_WBUF, d_model, d_ff), bf16),
+            pltpu.VMEM((N_WBUF, d_ff, d_model), bf16),
+            pltpu.VMEM((N_SEG, SEG_ROWS, d_model), bf16),
+            pltpu.VMEM((N_SEG, SEG_ROWS, d_model), bf16),
+            pltpu.VMEM((SLOT_ROWS, d_model), bf16),
+            pltpu.VMEM((SLOT_ROWS, d_model), jnp.float32),
+            pltpu.VMEM((LOCAL_ROWS, d_model), bf16),
+            pltpu.VMEM((N_SEG, SEG_ROWS, d_model), bf16),
+            pltpu.VMEM((N_SEG, SEG_ROWS, d_model), bf16),
+            pltpu.VMEM((8, n_tok), jnp.int32),
+            pltpu.VMEM((n_tok, 128), jnp.int32),
+            pltpu.SemaphoreType.DMA((n_slot, 2)),
+            pltpu.SemaphoreType.DMA((N_SEG, 3)),
+            pltpu.SemaphoreType.DMA((N_SEG, 3)),
+            pltpu.SemaphoreType.DMA((N_SEG, 3)),
+            pltpu.SemaphoreType.DMA((N_SEG, 3)),
+        ],
+        compiler_params=pltpu.CompilerParams(collective_id=0, has_side_effects=True, vmem_limit_bytes=60 * 1024 * 1024),
+    )(slot_expert, tokens, topk_idx.reshape(1, n_tok), w_up[0], w_down[0])
+
+
 def solution(mesh):
     def group_layer(tokens, topk_idx, topk_w, w_up, w_down, slot_expert):
-        n_tok, d_model = tokens.shape
-        n_top = topk_idx.shape[1]
-        n_dev, n_slot = slot_expert.shape
-        capacity = slot_bound(n_tok, n_top, n_dev, n_slot)
-        pair_pos, buf_tok = route_pairs(topk_idx, slot_expert, capacity)
-        send_buf = tokens[buf_tok].reshape(n_slot, n_dev, capacity, d_model)
-        recv_buf = lax.all_to_all(send_buf, 'ep', 1, 1, tiled=True)
-        expert_out = expert_ffn(recv_buf, w_up[0], w_down[0])
-        back_buf = lax.all_to_all(expert_out, 'ep', 1, 1, tiled=True)
-        pair_out = back_buf.reshape(-1, d_model)[pair_pos].reshape(n_tok, n_top, d_model)
-        mixed_out = jnp.sum(pair_out.astype(jnp.float32) * topk_w[:, :, None], axis=1)
-        return mixed_out.astype(jnp.bfloat16)
+        flat = slot_expert.reshape(-1)
+        copies = jnp.sum(flat[:, None] == flat[None, :], axis=1)
+        pair_out = lax.cond(jnp.any(copies == 4), fast_layer, general_layer, tokens, topk_idx, w_up, w_down, slot_expert)
+        return (pair_out.astype(jnp.float32) * topk_w).astype(jnp.bfloat16)
 
     row_spec = P(('dp', 'ep'), None)
     weight_spec = P('ep', None, None, None)

time: 173 us -> 57.7 us (0.33)
  Pallas kernels: 0 us -> 52.1 us
  local copies, waits for them, and re-layouts: 46.7 us -> 0.77 us
  matrix products: 38 us -> 0 us
  blocking collectives: 33.9 us -> 0 us
  waiting for transfers between devices: 29.3 us -> 0 us
  other arithmetic: 19.9 us -> 3.7 us
  starting transfers between devices: 4.51 us -> 0 us
    pallas_call x0 -> x1, Pallas kernels: none -> 52.1 us  [fast_layer(): pl.pallas_call(layer_kernel, out_shape=jax.ShapeDtypeStruct((n_tok, d_mod...]
    dot_general x2 -> x0, matrix products: 38 us -> none  [the longest x1 21.2 us: expert_ffn(): jnp.einsum('spcf,sfm->spcm', hidden, down_local, preferred_element_type=j...]
    all_to_all x1 -> x0, blocking collectives: 33.9 us -> none  [group_layer(): recv_buf = lax.all_to_all(send_buf, 'ep', 1, 1, tiled=True)]
    all_to_all x1 -> x0, waiting for transfers between devices: 29.3 us -> none  [group_layer(): back_buf = lax.all_to_all(expert_out, 'ep', 1, 1, tiled=True)]
    gather x4 -> x0, local copies, waits for them, and re-layouts: 22.3 us -> none  [the longest x1 8.86 us: route_pairs(): slot_flat = slot_of[flat_exp, pair_rank % pair_copies]]
    gather x5 -> x0, other arithmetic: 10.8 us -> none  [the longest x3 10.8 us: route_pairs(): pair_copies = exp_copies[flat_exp]]
    reshape x4 -> x0, local copies, waits for them, and re-layouts: 10.3 us -> none  [the longest x2 5.67 us: group_layer(): send_buf = tokens[buf_tok].reshape(n_slot, n_dev, capacity, d_model)]
    scatter x2 -> x0, local copies, waits for them, and re-layouts: 6.34 us -> none  [the longest x1 4.32 us: route_pairs(): jnp.zeros((n_slot * n_dev * capacity,), jnp.int32).at[pair_pos]]
  transfers between devices with their start and end apart: 1 -> 0, of which waited for: 1 -> 0; matrix products, arithmetic and copies ran while one was open for 0% -> 0% of each run, Pallas kernels for 0% -> 0%
where the time goes in v1:
time: 57.7 us; the launch traced here: 57.5 us
  Pallas kernels  52.1 us (90%)
  other arithmetic  3.7 us (6%)
  local copies, waits for them, and re-layouts  0.77 us (1%)
  between operations  0.68 us (1%)
    pallas_call x1, Pallas kernels, fast_layer(): pl.pallas_call(layer_kernel, out_shape=jax.ShapeDtypeStruct((n_tok, d_mod...  52.1 us
    convert_element_type x1, other arithmetic, group_layer(): return (pair_out.astype(jnp.float32) * topk_w).astype(jnp.bfloat16)  2.87 us

profile of v1, /device:TPU:0, one launch (start us, length us, event | category | flops | bytes accessed | tf_op | source)
XLA Modules:
  0.0 57.5 jit_solution(2843653730007559196)
XLA Ops:
  0.0 0.8 %eq.71 = s32[20]{0:T(128)S(1)} reshape(s32[4,5]{1,0:T(4,128)} %param.13) | data formatting | bytes 160 | tf_op jit(solution)/shard_map/eq | solution.py:272
  0.8 0.2 convert_reduce_fusion.1
  0.9 0.6 %compare_reduce_fusion.9 = pred[]{:T(512)} fusion(s32[20]{0:T(128)S(1)} %convert_reduce_fusion.1), kind=kLoop, calls=%fused_computation.88 | loop fusion | flops 39 | bytes 81 | tf_op jit(solution)/shard_map/reduce_or | solution.py:273
  2.2 0.0 copy-start.1
  2.3 52.4 %conditional.6 = (bf16[1024,768]{1,0:T(8,128)(2,1)}) conditional(s32[]{:T(128)} %convert_element_type.35, (s32[4,5]{1,0:T(4,128)}, s32[1024,1]{0,1:T(1,128)}, bf16[1024,768]{1,0:T(8,128)(2,1)}, bf16[1,5,768,3072]{3,2,1,0:T(8,128)(2,1)}, bf16[1,5,3072,768]{3,2,1,0:T(8,128)(2,1)}) %tuple.21, (s32[1024,1]{0,1:T(1,128)}, ...), branch_computations={%region_2.10_spmd, %region_10.11_spmd} | conditional | flops 14579325952 | bytes 140180960
  2.5 52.1 %branch_1_fun.1 = bf16[1024,768]{1,0:T(8,128)(2,1)} custom-call(s32[4,5]{1,0:T(4,128)} %get-tuple-element.39.table, bf16[1024,768]{1,0:T(8,128)(2,1)} %get-tuple-element.40.tokens, s32[1,1024]{1,0:T(1,128)} %bitcast.75, bf16[5,768,3072]{2,1,0:T(8,128)(2,1)} %bitcast.70, bf16[5,3072,768]{2,1,0:T(8,128)(2,1)} %bitcast.71), custom_call_target="tpu_custom_call" | custom-call | tf_op jit(solution)/shard_map/cond/branch_1_fun/pallas_call | solution.py:242
  54.6 0.0 copy-done.1
  54.6 2.9 %multiply_convert_fusion = bf16[1024,768]{1,0:T(8,128)(2,1)} fusion(bf16[1024,768]{1,0:T(8,128)(2,1)} %get-tuple-element.73, f32[1024]{0:T(1024)S(1)} %bitcast.86), kind=kLoop, calls=%fused_computation.86 | loop fusion | flops 2359296 | bytes 3149824 | tf_op jit(solution)/shard_map/convert_element_type | solution.py:274
Async XLA Ops:
  2.2 52.4 %copy-start.1 = (f32[1024,1]{0,1:T(1,128)S(1)}, f32[1024,1]{0,1:T(1,128)}, u32[]{:S(2)}) copy-start(f32[1024,1]{0,1:T(1,128)} %param.10) | copy-start | bytes 12292

commit v2 on v1

--- a/solution.py
+++ b/solution.py
@@ -53,7 +53,7 @@
     return jnp.einsum('spcf,sfm->spcm', hidden, down_local, preferred_element_type=jnp.float32).astype(jnp.bfloat16)
 
 
-def general_layer(tokens, topk_idx, w_up, w_down, slot_expert):
+def general_layer(tokens, topk_idx, topk_w, w_up, w_down, slot_expert):
     n_tok, d_model = tokens.shape
     n_top = topk_idx.shape[1]
     n_dev, n_slot = slot_expert.shape
@@ -63,7 +63,8 @@
     recv_buf = lax.all_to_all(send_buf, 'ep', 1, 1, tiled=True)
     expert_out = expert_ffn(recv_buf, w_up[0], w_down[0])
     back_buf = lax.all_to_all(expert_out, 'ep', 1, 1, tiled=True)
-    return back_buf.reshape(-1, d_model)[pair_pos]
+    pair_out = back_buf.reshape(-1, d_model)[pair_pos]
+    return (pair_out.astype(jnp.float32) * topk_w).astype(jnp.bfloat16)
 
 
 def route(idx_row, table, peers, n_exp, n_slot):
@@ -116,9 +117,9 @@
     return code.astype(jnp.int32), hot_slot
 
 
-def layer_kernel(table, tokens, idx_row, w_up, w_down, out, up_buf, down_buf, send, recv, x_buf, acc, result, back_send, back_recv, code_row, code_col, w_sem, ds_sem, dr_sem, bs_sem, br_sem):
+def layer_kernel(table, idx_row, gate_row, tokens, w_up, w_down, out, found, tok_buf, up_buf, down_buf, send, recv, acc, rows_buf, back_send, back_recv, mixed, code_row, code_col, gate_col, t_sem, w_sem, ds_sem, dr_sem, bs_sem, br_sem, o_sem):
     f32, bf16 = jnp.float32, jnp.bfloat16
-    n_tok, d_model = tokens.shape
+    n_tok, d_model = tok_buf.shape
     n_slot = w_up.shape[0]
     d_ff = w_up.shape[2]
     me = lax.axis_index('ep')
@@ -134,21 +135,20 @@
         return (pltpu.make_async_copy(w_up.at[s], up_buf.at[b], w_sem.at[s, 0]),
                 pltpu.make_async_copy(w_down.at[s], down_buf.at[b], w_sem.at[s, 1]))
 
+    token_copy = pltpu.make_async_copy(tokens, tok_buf, t_sem)
+    token_copy.start()
     for s in range(N_WBUF):
         for copy in weight_copies(s):
             copy.start()
 
     code, hot_slot = route(idx_row[...], table, peers, 16, n_slot)
     code_row[...] = jnp.broadcast_to(code, code_row.shape)
-    code_col[...] = jnp.transpose(jnp.broadcast_to(code, (128, n_tok)))
     hot_slot = hot_slot[:, :1]
-    back_recv[:, 3 * SEG:, :] = jnp.zeros((N_SEG, SEG_ROWS - 3 * SEG, d_model), bf16)
-    result[n_slot * SLOT_ROWS:, :] = jnp.zeros((LOCAL_ROWS - n_slot * SLOT_ROWS, d_model), bf16)
 
     def pick(first, rows):
         ids = lax.broadcasted_iota(jnp.int32, (rows, n_tok), 0) + first
         mask = (ids == code_row[0:1, :]).astype(f32).astype(bf16)
-        return jnp.dot(mask, tokens[...], preferred_element_type=f32).astype(bf16)
+        return jnp.dot(mask, tok_buf[...], preferred_element_type=f32).astype(bf16)
 
     def dispatch_copy(k, r):
         rows = pl.ds((r - 1) * SEG, SEG)
@@ -164,6 +164,7 @@
             send_sem=bs_sem.at[k, r - 1], recv_sem=br_sem.at[k, r - 1],
             device_id={'ep': peers[r]}, device_id_type=MESH)
 
+    token_copy.wait()
     for k in range(N_SEG):
         send[k] = pick(k * SEG_ROWS, SEG_ROWS)
         if k == 0:
@@ -172,16 +173,28 @@
             dispatch_copy(k, r).start()
 
     for s in range(n_slot):
-        x_buf[...] = pick(LOCAL_BASE + s * SLOT_ROWS, SLOT_ROWS)
+        rows_buf[s * SLOT_ROWS:(s + 1) * SLOT_ROWS, :] = pick(LOCAL_BASE + s * SLOT_ROWS, SLOT_ROWS)
+    code_col[...] = jnp.transpose(jnp.broadcast_to(code, (128, n_tok)))
+    gate_col[...] = jnp.transpose(jnp.broadcast_to(gate_row[...], (128, n_tok)))
+    back_recv[:, 3 * SEG:, :] = jnp.zeros((N_SEG, SEG_ROWS - 3 * SEG, d_model), bf16)
+    rows_buf[n_slot * SLOT_ROWS:, :] = jnp.zeros((LOCAL_ROWS - n_slot * SLOT_ROWS, d_model), bf16)
+    hot = jnp.int32(0)
+    for s in range(n_slot):
+        here = sum((table[d, q] == table[me, s]).astype(jnp.int32) for d in range(4) for q in range(n_slot))
+        hot = hot | (here == 4).astype(jnp.int32)
+    found[0, 0] = hot
+
+    for s in range(n_slot):
+        lo, hi = s * SLOT_ROWS, (s + 1) * SLOT_ROWS
         if s < N_SEG:
             for r in (1, 2, 3):
                 dispatch_copy(s, r).wait_recv()
-        far = x_buf[SEG:, :].astype(f32)
+        far = rows_buf[lo + SEG:hi, :].astype(f32)
         if s < N_SEG:
             far = far + recv[s, :3 * SEG, :].astype(f32) * (hot_slot > s).astype(f32)
         if s > 0:
             far = far + recv[s - 1, :3 * SEG, :].astype(f32) * (hot_slot < s).astype(f32)
-        x_buf[SEG:, :] = far.astype(bf16)
+        rows_buf[lo + SEG:hi, :] = far.astype(bf16)
         for copy in weight_copies(s):
             copy.wait()
         b = s % N_WBUF
@@ -189,7 +202,7 @@
 
         def ff_step(i, carry):
             cols = pl.ds(pl.multiple_of(i * FF_TILE, FF_TILE), FF_TILE)
-            pre = jnp.dot(x_buf[...], up_buf[b, :, cols], preferred_element_type=f32)
+            pre = jnp.dot(rows_buf[lo:hi, :], up_buf[b, :, cols], preferred_element_type=f32)
             hidden = jax.nn.gelu(pre, approximate=True).astype(bf16)
             acc[...] += jnp.dot(hidden, down_buf[b, cols, :], preferred_element_type=f32)
             return carry
@@ -198,18 +211,24 @@
         if s + N_WBUF < n_slot:
             for copy in weight_copies(s + N_WBUF):
                 copy.start()
-        result[s * SLOT_ROWS:(s + 1) * SLOT_ROWS, :] = acc[...].astype(bf16)
+        rows_buf[lo:hi, :] = acc[...].astype(bf16)
         if s > 0:
             k = s - 1
-            prev = result[k * SLOT_ROWS + SEG:(k + 1) * SLOT_ROWS, :].astype(f32)
-            back = prev * (hot_slot > k).astype(f32) + acc[SEG:, :].astype(bf16).astype(f32) * (hot_slot <= k).astype(f32)
+            prev = rows_buf[lo - SLOT_ROWS + SEG:lo, :].astype(f32)
+            last = rows_buf[lo + SEG:hi, :].astype(f32)
+            back = prev * (hot_slot > k).astype(f32) + last * (hot_slot <= k).astype(f32)
             back_send[k, :3 * SEG, :] = back.astype(bf16)
             for r in (2, 3, 1):
                 back_copy(k, r).start()
 
     tile = 256
-
-    def combine(first, rows, source, add):
+    n_tile = n_tok // tile
+
+    def out_copy(i):
+        at = pl.ds(pl.multiple_of(i * tile, tile), tile)
+        return pltpu.make_async_copy(mixed.at[at], out.at[at], o_sem.at[i])
+
+    def combine(first, rows, source, add, final):
         def body(i, carry):
             at = pl.ds(pl.multiple_of(i * tile, tile), tile)
             mine = code_col[at, :]
@@ -217,61 +236,71 @@
             mask = jnp.concatenate([(mine == ids + 128 * j).astype(f32).astype(bf16) for j in range(rows // 128)], axis=1)
             part = jnp.dot(mask, source(), preferred_element_type=f32)
             if add:
-                part = part + out[at, :].astype(f32)
-            out[at, :] = part.astype(bf16)
+                part = part + mixed[at, :].astype(f32)
+            if final:
+                part = part * jnp.concatenate([gate_col[at, :]] * (d_model // 128), axis=1)
+            mixed[at, :] = part.astype(bf16)
+            if final:
+                out_copy(i).start()
             return carry
-        lax.fori_loop(0, n_tok // tile, body, 0)
-
-    combine(LOCAL_BASE, LOCAL_ROWS, lambda: result[...], False)
+        lax.fori_loop(0, n_tile, body, 0)
+
+    combine(LOCAL_BASE, LOCAL_ROWS, lambda: rows_buf[...], False, False)
     for k in range(N_SEG):
         for r in (1, 2, 3):
             back_copy(k, r).wait_recv()
-        combine(k * SEG_ROWS, SEG_ROWS, lambda: back_recv[k], True)
+        combine(k * SEG_ROWS, SEG_ROWS, lambda: back_recv[k], True, k == N_SEG - 1)
     for k in range(N_SEG):
         for r in (1, 2, 3):
             dispatch_copy(k, r).wait_send()
             back_copy(k, r).wait_send()
-
-
-def fast_layer(tokens, topk_idx, w_up, w_down, slot_expert):
+    for i in range(n_tile):
+        out_copy(i).wait()
+
+
+def fast_layer(tokens, topk_idx, topk_w, w_up, w_down, slot_expert):
     n_tok, d_model = tokens.shape
     n_slot, d_ff = w_up.shape[1], w_up.shape[3]
     vmem = pl.BlockSpec(memory_space=pltpu.VMEM)
+    smem = pl.BlockSpec(memory_space=pltpu.SMEM)
     anym = pl.BlockSpec(memory_space=pl.ANY)
     bf16 = jnp.bfloat16
     return pl.pallas_call(
         layer_kernel,
-        out_shape=jax.ShapeDtypeStruct((n_tok, d_model), bf16),
-        in_specs=[pl.BlockSpec(memory_space=pltpu.SMEM), vmem, vmem, anym, anym],
-        out_specs=vmem,
+        out_shape=(jax.ShapeDtypeStruct((n_tok, d_model), bf16), jax.ShapeDtypeStruct((1, 1), jnp.int32)),
+        in_specs=[smem, vmem, vmem, anym, anym, anym],
+        out_specs=(anym, smem),
         scratch_shapes=[
+            pltpu.VMEM((n_tok, d_model), bf16),
             pltpu.VMEM((N_WBUF, d_model, d_ff), bf16),
             pltpu.VMEM((N_WBUF, d_ff, d_model), bf16),
             pltpu.VMEM((N_SEG, SEG_ROWS, d_model), bf16),
             pltpu.VMEM((N_SEG, SEG_ROWS, d_model), bf16),
-            pltpu.VMEM((SLOT_ROWS, d_model), bf16),
             pltpu.VMEM((SLOT_ROWS, d_model), jnp.float32),
             pltpu.VMEM((LOCAL_ROWS, d_model), bf16),
             pltpu.VMEM((N_SEG, SEG_ROWS, d_model), bf16),
             pltpu.VMEM((N_SEG, SEG_ROWS, d_model), bf16),
+            pltpu.VMEM((n_tok, d_model), bf16),
             pltpu.VMEM((8, n_tok), jnp.int32),
             pltpu.VMEM((n_tok, 128), jnp.int32),
+            pltpu.VMEM((n_tok, 128), jnp.float32),
+            pltpu.SemaphoreType.DMA,
             pltpu.SemaphoreType.DMA((n_slot, 2)),
             pltpu.SemaphoreType.DMA((N_SEG, 3)),
             pltpu.SemaphoreType.DMA((N_SEG, 3)),
             pltpu.SemaphoreType.DMA((N_SEG, 3)),
             pltpu.SemaphoreType.DMA((N_SEG, 3)),
+            pltpu.SemaphoreType.DMA((n_tok // 256,)),
         ],
         compiler_params=pltpu.CompilerParams(collective_id=0, has_side_effects=True, vmem_limit_bytes=60 * 1024 * 1024),
-    )(slot_expert, tokens, topk_idx.reshape(1, n_tok), w_up[0], w_down[0])
+    )(slot_expert, topk_idx.reshape(1, n_tok), topk_w.reshape(1, n_tok), tokens, w_up[0], w_down[0])
 
 
 def solution(mesh):
     def group_layer(tokens, topk_idx, topk_w, w_up, w_down, slot_expert):
-        flat = slot_expert.reshape(-1)
-        copies = jnp.sum(flat[:, None] == flat[None, :], axis=1)
-        pair_out = lax.cond(jnp.any(copies == 4), fast_layer, general_layer, tokens, topk_idx, w_up, w_down, slot_expert)
-        return (pair_out.astype(jnp.float32) * topk_w).astype(jnp.bfloat16)
+        fast_out, found = fast_layer(tokens, topk_idx, topk_w, w_up, w_down, slot_expert)
+        args = (fast_out, tokens, topk_idx, topk_w, w_up, w_down, slot_expert)
+        return lax.cond(found[0, 0] == 1, lambda *a: a[0], lambda *a: general_layer(*a[1:]), *args)
 
     row_spec = P(('dp', 'ep'), None)
     weight_spec = P('ep', None, None, None)

time: 57.7 us -> 63.2 us (1.095)
  Pallas kernels: 52.1 us -> 59.7 us
  other arithmetic: 3.7 us -> 0 us
  local copies, waits for them, and re-layouts: 0.77 us -> 2.67 us
    pallas_call x1, Pallas kernels: 52.1 us -> 59.7 us  [fast_layer(): pl.pallas_call(layer_kernel, out_shape=(jax.ShapeDtypeStruct((n_tok, d_mo...]
    convert_element_type x1 -> x0, other arithmetic: 2.87 us -> none  [group_layer(): return (pair_out.astype(jnp.float32) * topk_w).astype(jnp.bfloat16)]
    unnamed x2 -> x9, local copies, waits for them, and re-layouts: 0.01 us -> 2.67 us
    eq x1 -> x0, local copies, waits for them, and re-layouts: 0.76 us -> none  [group_layer(): copies = jnp.sum(flat[:, None] == flat[None, :], axis=1)]
    reduce_or x1 -> x0, other arithmetic: 0.64 us -> none  [group_layer(): jnp.any(copies == 4)]
where the time goes in v2:
time: 63.2 us; the launch traced here: 63.1 us
  Pallas kernels  59.7 us (94%)
  local copies, waits for them, and re-layouts  2.67 us (4%)
  between operations  0.74 us (1%)
    pallas_call x1, Pallas kernels, fast_layer(): pl.pallas_call(layer_kernel, out_shape=(jax.ShapeDtypeStruct((n_tok, d_mo...  59.7 us
    unnamed x9, local copies, waits for them, and re-layouts  2.67 us

profile of v2, /device:TPU:0, one launch (start us, length us, event | category | flops | bytes accessed | tf_op | source)
XLA Modules:
  0.0 63.1 jit_solution(17544867409182620588)
XLA Ops:
  0.0 0.0 copy-start
  0.0 0.0 copy-start.1
  0.0 0.0 copy-start.2
  0.0 0.0 copy-start.3
  0.0 59.7 %shard_map.66 = (bf16[1024,768]{1,0:T(8,128)(2,1)}, s32[1,1]{1,0:T(1,128)}) custom-call(s32[4,5]{1,0:T(4,128)} %table.1, s32[1,1024]{1,0:T(1,128)} %bitcast.75, f32[1,1024]{1,0:T(1,128)} %bitcast.82, bf16[1024,768]{1,0:T(8,128)(2,1)} %tokens.1, bf16[5,768,3072]{2,1,0:T(8,128)(2,1)} %bitcast.72, bf16[5,3072,768]{2,1,0:T(8,128)(2,1)} %bitcast.73), custom_call_target="tpu_custom_call" | custom-call | tf_op jit(solution)/shard_map/pallas_call | solution.py:268
  60.4 0.0 copy-done
  60.4 0.0 copy-done.1
  60.4 0.0 copy-done.2
  60.4 0.0 copy-done.3
  60.5 2.7 %copy.35 = bf16[1024,768]{1,0:T(8,128)(2,1)} copy(bf16[1024,768]{1,0:T(8,128)(2,1)} %get-tuple-element.31) | data formatting | bytes 3145728
  (1 shorter events, 0.0 us)
Async XLA Ops:
  0.0 60.4 %copy-start = (bf16[1024,768]{1,0:T(8,128)(2,1)S(1)}, bf16[1024,768]{1,0:T(8,128)(2,1)}, u32[]{:S(2)}) copy-start(bf16[1024,768]{1,0:T(8,128)(2,1)} %tokens.1) | copy-start | bytes 4718596
  0.0 60.4 %copy-start.1 = (s32[1024,1]{0,1:T(1,128)S(1)}, s32[1024,1]{0,1:T(1,128)}, u32[]{:S(2)}) copy-start(s32[1024,1]{0,1:T(1,128)} %param.9) | copy-start | bytes 12292
  0.0 60.4 %copy-start.2 = (s32[4,5]{1,0:T(4,128)S(1)}, s32[4,5]{1,0:T(4,128)}, u32[]{:S(2)}) copy-start(s32[4,5]{1,0:T(4,128)} %table.1) | copy-start | bytes 244
  0.0 60.4 %copy-start.3 = (f32[1024,1]{0,1:T(1,128)S(1)}, f32[1024,1]{0,1:T(1,128)}, u32[]{:S(2)}) copy-start(f32[1024,1]{0,1:T(1,128)} %param.10) | copy-start | bytes 12292

commit v3 on v2

--- a/solution.py
+++ b/solution.py
@@ -114,10 +114,10 @@
     for c in range(MAX_COPIES - 1):
         start = jnp.where(which == c, wide(base[c]), start)
     code = jnp.sum(onehot * (start + row), axis=0, keepdims=True)
-    return code.astype(jnp.int32), hot_slot
-
-
-def layer_kernel(table, idx_row, gate_row, tokens, w_up, w_down, out, found, tok_buf, up_buf, down_buf, send, recv, acc, rows_buf, back_send, back_recv, mixed, code_row, code_col, gate_col, t_sem, w_sem, ds_sem, dr_sem, bs_sem, br_sem, o_sem):
+    return code.astype(jnp.int32), hot_slot, jnp.max(own * hot, axis=0, keepdims=True)
+
+
+def layer_kernel(slot_expert, topk_idx, topk_w, tokens, w_up, w_down, out, last_rows, last_mask, last_gate, found, table, idx_row, gate_row, tok_buf, up_buf, down_buf, send, recv, acc, rows_buf, back_send, back_recv, mixed, mask_buf, gate_buf, code_row, code_col, gate_col, t_sem, w_sem, ds_sem, dr_sem, bs_sem, br_sem, o_sem):
     f32, bf16 = jnp.float32, jnp.bfloat16
     n_tok, d_model = tok_buf.shape
     n_slot = w_up.shape[0]
@@ -135,13 +135,16 @@
         return (pltpu.make_async_copy(w_up.at[s], up_buf.at[b], w_sem.at[s, 0]),
                 pltpu.make_async_copy(w_down.at[s], down_buf.at[b], w_sem.at[s, 1]))
 
-    token_copy = pltpu.make_async_copy(tokens, tok_buf, t_sem)
+    small_copies = [pltpu.make_async_copy(slot_expert, table, t_sem.at[0]),
+                    pltpu.make_async_copy(topk_idx, idx_row, t_sem.at[1]),
+                    pltpu.make_async_copy(topk_w, gate_row, t_sem.at[2])]
+    token_copy = pltpu.make_async_copy(tokens, tok_buf, t_sem.at[3])
+    for copy in small_copies:
+        copy.start()
     token_copy.start()
-    for s in range(N_WBUF):
-        for copy in weight_copies(s):
-            copy.start()
-
-    code, hot_slot = route(idx_row[...], table, peers, 16, n_slot)
+    for copy in small_copies:
+        copy.wait()
+    code, hot_slot, hot_here = route(idx_row[...], table, peers, 16, n_slot)
     code_row[...] = jnp.broadcast_to(code, code_row.shape)
     hot_slot = hot_slot[:, :1]
 
@@ -160,11 +163,14 @@
     def back_copy(k, r):
         rows = pl.ds((r - 1) * SEG, SEG)
         return pltpu.make_async_remote_copy(
-            src_ref=back_send.at[k, rows], dst_ref=back_recv.at[k, rows],
+            src_ref=back_send.at[k, rows], dst_ref=back_recv.at[k, rows] if k < N_SEG - 1 else last_rows.at[rows],
             send_sem=bs_sem.at[k, r - 1], recv_sem=br_sem.at[k, r - 1],
             device_id={'ep': peers[r]}, device_id_type=MESH)
 
     token_copy.wait()
+    for s in range(N_WBUF):
+        for copy in weight_copies(s):
+            copy.start()
     for k in range(N_SEG):
         send[k] = pick(k * SEG_ROWS, SEG_ROWS)
         if k == 0:
@@ -176,13 +182,20 @@
         rows_buf[s * SLOT_ROWS:(s + 1) * SLOT_ROWS, :] = pick(LOCAL_BASE + s * SLOT_ROWS, SLOT_ROWS)
     code_col[...] = jnp.transpose(jnp.broadcast_to(code, (128, n_tok)))
     gate_col[...] = jnp.transpose(jnp.broadcast_to(gate_row[...], (128, n_tok)))
-    back_recv[:, 3 * SEG:, :] = jnp.zeros((N_SEG, SEG_ROWS - 3 * SEG, d_model), bf16)
+    back_recv[:, 3 * SEG:, :] = jnp.zeros((N_SEG - 1, SEG_ROWS - 3 * SEG, d_model), bf16)
     rows_buf[n_slot * SLOT_ROWS:, :] = jnp.zeros((LOCAL_ROWS - n_slot * SLOT_ROWS, d_model), bf16)
-    hot = jnp.int32(0)
-    for s in range(n_slot):
-        here = sum((table[d, q] == table[me, s]).astype(jnp.int32) for d in range(4) for q in range(n_slot))
-        hot = hot | (here == 4).astype(jnp.int32)
-    found[0, 0] = hot
+    found[...] = jnp.broadcast_to(hot_here.astype(jnp.int32), found.shape)
+    last = (N_SEG - 1) * SEG_ROWS
+    ids = lax.broadcasted_iota(jnp.int32, (3 * SEG, n_tok), 0) + last
+    gates = jnp.sum(jnp.where(ids == code_row[0:1, :], gate_row[...], 0.0), axis=1, keepdims=True)
+    gate_buf[...] = jnp.broadcast_to(gates, gate_buf.shape)
+    ids = lax.broadcasted_iota(jnp.int32, (n_tok, 128), 1) + last
+    for j in range(SEG_ROWS // 128):
+        mask_buf[:, j * 128:(j + 1) * 128] = (code_col[...] == ids + 128 * j).astype(f32).astype(bf16)
+    side_copies = [pltpu.make_async_copy(mask_buf, last_mask, t_sem.at[4]),
+                   pltpu.make_async_copy(gate_buf, last_gate, t_sem.at[5])]
+    for copy in side_copies:
+        copy.start()
 
     for s in range(n_slot):
         lo, hi = s * SLOT_ROWS, (s + 1) * SLOT_ROWS
@@ -249,28 +262,60 @@
     for k in range(N_SEG):
         for r in (1, 2, 3):
             back_copy(k, r).wait_recv()
-        combine(k * SEG_ROWS, SEG_ROWS, lambda: back_recv[k], True, k == N_SEG - 1)
+        if k < N_SEG - 1:
+            combine(k * SEG_ROWS, SEG_ROWS, lambda: back_recv[k], True, k == N_SEG - 2)
+        if k == N_SEG - 2:
+            for i in range(n_tile):
+                out_copy(i).wait()
+            for copy in side_copies:
+                copy.wait()
     for k in range(N_SEG):
         for r in (1, 2, 3):
             dispatch_copy(k, r).wait_send()
             back_copy(k, r).wait_send()
-    for i in range(n_tile):
-        out_copy(i).wait()
+
+
+def last_kernel(part, rows, mask, gate, out):
+    f32, bf16 = jnp.float32, jnp.bfloat16
+    d_model = part.shape[1]
+    gates = jnp.concatenate([gate[...]] * (d_model // 128), axis=1)
+    scaled = (rows[...].astype(f32) * gates).astype(bf16)
+    scaled = jnp.concatenate([scaled, jnp.zeros((SEG_ROWS - scaled.shape[0], d_model), bf16)], axis=0)
+    late = jnp.dot(mask[...], scaled, preferred_element_type=f32)
+    out[...] = (late + part[...].astype(f32)).astype(bf16)
+
+
+def add_last(part, rows, mask, gate):
+    n_tok, d_model = part.shape
+    tile = 256
+    by_tile = lambda cols: pl.BlockSpec((tile, cols), lambda i: (i, 0))
+    whole = lambda a: pl.BlockSpec(a.shape, lambda i: (0, 0))
+    return pl.pallas_call(
+        last_kernel,
+        grid=(n_tok // tile,),
+        out_shape=jax.ShapeDtypeStruct(part.shape, part.dtype),
+        in_specs=[by_tile(d_model), whole(rows), by_tile(mask.shape[1]), whole(gate)],
+        out_specs=by_tile(d_model),
+    )(part, rows, mask, gate)
 
 
 def fast_layer(tokens, topk_idx, topk_w, w_up, w_down, slot_expert):
     n_tok, d_model = tokens.shape
     n_slot, d_ff = w_up.shape[1], w_up.shape[3]
     vmem = pl.BlockSpec(memory_space=pltpu.VMEM)
-    smem = pl.BlockSpec(memory_space=pltpu.SMEM)
     anym = pl.BlockSpec(memory_space=pl.ANY)
     bf16 = jnp.bfloat16
     return pl.pallas_call(
         layer_kernel,
-        out_shape=(jax.ShapeDtypeStruct((n_tok, d_model), bf16), jax.ShapeDtypeStruct((1, 1), jnp.int32)),
-        in_specs=[smem, vmem, vmem, anym, anym, anym],
-        out_specs=(anym, smem),
+        out_shape=(jax.ShapeDtypeStruct((n_tok, d_model), bf16), jax.ShapeDtypeStruct((3 * SEG, d_model), bf16),
+                   jax.ShapeDtypeStruct((n_tok, SEG_ROWS), bf16), jax.ShapeDtypeStruct((3 * SEG, 128), jnp.float32),
+                   jax.ShapeDtypeStruct((1, 128), jnp.int32)),
+        in_specs=[anym] * 6,
+        out_specs=(anym, anym, anym, anym, vmem),
         scratch_shapes=[
+            pltpu.SMEM(slot_expert.shape, jnp.int32),
+            pltpu.VMEM((1, n_tok), jnp.int32),
+            pltpu.VMEM((1, n_tok), jnp.float32),
             pltpu.VMEM((n_tok, d_model), bf16),
             pltpu.VMEM((N_WBUF, d_model, d_ff), bf16),
             pltpu.VMEM((N_WBUF, d_ff, d_model), bf16),
@@ -279,12 +324,14 @@
             pltpu.VMEM((SLOT_ROWS, d_model), jnp.float32),
             pltpu.VMEM((LOCAL_ROWS, d_model), bf16),
             pltpu.VMEM((N_SEG, SEG_ROWS, d_model), bf16),
-            pltpu.VMEM((N_SEG, SEG_ROWS, d_model), bf16),
+            pltpu.VMEM((N_SEG - 1, SEG_ROWS, d_model), bf16),
             pltpu.VMEM((n_tok, d_model), bf16),
+            pltpu.VMEM((n_tok, SEG_ROWS), bf16),
+            pltpu.VMEM((3 * SEG, 128), jnp.float32),
             pltpu.VMEM((8, n_tok), jnp.int32),
             pltpu.VMEM((n_tok, 128), jnp.int32),
             pltpu.VMEM((n_tok, 128), jnp.float32),
-            pltpu.SemaphoreType.DMA,
+            pltpu.SemaphoreType.DMA((6,)),
             pltpu.SemaphoreType.DMA((n_slot, 2)),
             pltpu.SemaphoreType.DMA((N_SEG, 3)),
             pltpu.SemaphoreType.DMA((N_SEG, 3)),
@@ -298,9 +345,9 @@
 
 def solution(mesh):
     def group_layer(tokens, topk_idx, topk_w, w_up, w_down, slot_expert):
-        fast_out, found = fast_layer(tokens, topk_idx, topk_w, w_up, w_down, slot_expert)
-        args = (fast_out, tokens, topk_idx, topk_w, w_up, w_down, slot_expert)
-        return lax.cond(found[0, 0] == 1, lambda *a: a[0], lambda *a: general_layer(*a[1:]), *args)
+        *parts, found = fast_layer(tokens, topk_idx, topk_w, w_up, w_down, slot_expert)
+        args = (*parts, tokens, topk_idx, topk_w, w_up, w_down, slot_expert)
+        return lax.cond(found[0, 0] == 1, lambda *a: add_last(*a[:4]), lambda *a: general_layer(*a[4:]), *args)
 
     row_spec = P(('dp', 'ep'), None)
     weight_spec = P('ep', None, None, None)

time: 63.2 us -> 53.7 us (0.85)
  Pallas kernels: 59.7 us -> 51.6 us
  local copies, waits for them, and re-layouts: 2.67 us -> 1.15 us
    pallas_call x1, Pallas kernels: 59.7 us -> 48.7 us  [fast_layer(): pl.pallas_call(layer_kernel, out_shape=(jax.ShapeDtypeStruct((n_tok, d_mo...]
    pallas_call x0 -> x1, Pallas kernels: none -> 2.87 us  [add_last(): pl.pallas_call(last_kernel, grid=(n_tok // tile,), out_shape=jax.ShapeDty...]
    unnamed x9 -> x10, local copies, waits for them, and re-layouts: 2.67 us -> 1.15 us
where the time goes in v3:
time: 53.7 us; the launch traced here: 53.5 us
  Pallas kernels  51.6 us (96%)
  local copies, waits for them, and re-layouts  1.15 us (2%)
  between operations  0.75 us (1%)
    pallas_call x1, Pallas kernels, fast_layer(): pl.pallas_call(layer_kernel, out_shape=(jax.ShapeDtypeStruct((n_tok, d_mo...  48.7 us
    pallas_call x1, Pallas kernels, add_last(): pl.pallas_call(last_kernel, grid=(n_tok // tile,), out_shape=jax.ShapeDty...  2.87 us
    unnamed x10, local copies, waits for them, and re-layouts  1.15 us

profile of v3, /device:TPU:0, one launch (start us, length us, event | category | flops | bytes accessed | tf_op | source)
XLA Modules:
  0.0 53.5 jit_solution(15542203438577840131)
XLA Ops:
  0.0 0.0 copy-start
  0.0 0.0 copy-start.2
  0.0 0.0 copy-start.3
  0.0 0.0 copy-start.4
  0.0 48.7 %shard_map.66 = (bf16[1024,768]{1,0:T(8,128)(2,1)}, bf16[240,768]{1,0:T(8,128)(2,1)S(1)}, bf16[1024,256]{1,0:T(8,128)(2,1)S(1)}, f32[240,128]{1,0:T(8,128)S(1)}, s32[1,128]{1,0:T(1,128)}) custom-call(s32[4,5]{1,0:T(4,128)} %slot_expert.1, s32[1,1024]{1,0:T(1,128)} %bitcast.76, f32[1,1024]{1,0:T(1,128)} %bitcast.83, bf16[1024,768]{1,0:T(8,128)(2,1)} %tokens.1, ...), custom_call_target="tpu_custom_call" | custom-call | tf_op jit(solution)/shard_map/pallas_call | solution.py:308
  49.5 0.0 copy-done
  49.5 0.0 copy-done.2
  49.5 0.0 copy-done.3
  49.5 0.0 copy-done.4
  49.5 2.9 %conditional.1 = (bf16[1024,768]{1,0:T(8,128)(2,1)S(1)}) conditional(s32[]{:T(128)} %bitcast.40, (s32[4,5]{1,0:T(4,128)S(1)}, s32[1024,1]{0,1:T(1,128)S(1)}, bf16[1024,768]{1,0:T(8,128)(2,1)S(1)}, bf16[1,5,768,3072]{3,2,1,0:T(8,128)(2,1)}, bf16[1,5,3072,768]{3,2,1,0:T(8,128)(2,1)}, /*index=5*/f32[1024,1]{0,1:T(1,128)S(1)}) %tuple.46, ...), branch_computations={%region_0.8_spmd, %region_8.9_spmd} | conditional | flops 14581685248 | bytes 137039296 | solution.py:350
  49.5 2.9 %branch_1_fun.1 = bf16[1024,768]{1,0:T(8,128)(2,1)S(1)} custom-call(bf16[1024,768]{1,0:T(8,128)(2,1)} %get-tuple-element.34.part, bf16[240,768]{1,0:T(8,128)(2,1)S(1)} %get-tuple-element.35.rows, bf16[1024,256]{1,0:T(8,128)(2,1)S(1)} %get-tuple-element.36.mask, f32[240,128]{1,0:T(8,128)S(1)} %get-tuple-element.37.gate), custom_call_target="tpu_custom_call" | custom-call | tf_op jit(solution)/shard_map/cond/branch_1_fun/pallas_call | solution.py:293
  52.4 0.0 copy-start.1
  52.4 1.1 %copy-done.1 = bf16[1024,768]{1,0:T(8,128)(2,1)} copy-done((bf16[1024,768]{1,0:T(8,128)(2,1)}, bf16[1024,768]{1,0:T(8,128)(2,1)S(1)}, u32[]{:S(2)}) %copy-start.1) | copy-done | bytes 1572888
Async XLA Ops:
  0.0 49.5 %copy-start = (bf16[1024,768]{1,0:T(8,128)(2,1)S(1)}, bf16[1024,768]{1,0:T(8,128)(2,1)}, u32[]{:S(2)}) copy-start(bf16[1024,768]{1,0:T(8,128)(2,1)} %tokens.1) | copy-start | bytes 4718596
  0.0 49.5 %copy-start.2 = (s32[1024,1]{0,1:T(1,128)S(1)}, s32[1024,1]{0,1:T(1,128)}, u32[]{:S(2)}) copy-start(s32[1024,1]{0,1:T(1,128)} %param.9) | copy-start | bytes 12292
  0.0 49.5 %copy-start.3 = (s32[4,5]{1,0:T(4,128)S(1)}, s32[4,5]{1,0:T(4,128)}, u32[]{:S(2)}) copy-start(s32[4,5]{1,0:T(4,128)} %slot_expert.1) | copy-start | bytes 244
  0.0 49.5 %copy-start.4 = (f32[1024,1]{0,1:T(1,128)S(1)}, f32[1024,1]{0,1:T(1,128)}, u32[]{:S(2)}) copy-start(f32[1024,1]{0,1:T(1,128)} %param.10) | copy-start | bytes 12292
  52.4 1.1 %copy-start.1 = (bf16[1024,768]{1,0:T(8,128)(2,1)}, bf16[1024,768]{1,0:T(8,128)(2,1)S(1)}, u32[]{:S(2)}) copy-start(bf16[1024,768]{1,0:T(8,128)(2,1)S(1)} %get-tuple-element.83) | copy-start | bytes 4718596

commit v4 on v3

v4 whole, which is shorter than its diff:
```python
import functools

import jax
import jax.numpy as jnp
from jax import lax
from jax.experimental import pallas as pl
from jax.experimental.pallas import tpu as pltpu
from jax.sharding import PartitionSpec as P

MAX_COPIES = 4
SEG = 80
N_SEG = 4
PAIR = 288
SEND_AT = (0, 80, 160, 240, 288)
BACK_AT = (0, 48, 128, 208, 288)
SLOT_ROWS = 4 * SEG
STREAM_AT = (None, 0, N_SEG * SEG, N_SEG * SEG + PAIR)
LOCAL_BASE = 1024
LOCAL_ROWS = 1664
LAST_ROWS = 256
EARLY_ROWS = 768
FF_TILE = 512
N_WBUF = 4
MESH = pl.DeviceIdType.MESH


def slot_bound(n_tok, n_top, n_dev, n_slot):
    base_load = (n_tok * n_top) // (n_dev * n_slot)
    return base_load + base_load // 2 + 1


def route_pairs(topk_idx, slot_expert, capacity):
    n_dev, n_slot = slot_expert.shape
    n_exp = n_dev * (n_slot - 1)
    n_top = topk_idx.shape[1]
    table_flat = slot_expert.reshape(-1)
    slot_ids = jnp.arange(n_dev * n_slot, dtype=jnp.int32)
    same_exp = table_flat[:, None] == table_flat[None, :]
    earlier = slot_ids[None, :] < slot_ids[:, None]
    copy_rank = jnp.sum(same_exp & earlier, axis=1, dtype=jnp.int32)
    exp_copies = jax.ops.segment_sum(jnp.ones_like(table_flat), table_flat, num_segments=n_exp)
    slot_of = jnp.zeros((n_exp, MAX_COPIES), jnp.int32).at[table_flat, copy_rank].set(slot_ids)
    flat_exp = topk_idx.reshape(-1)
    onehot = (flat_exp[:, None] == jnp.arange(n_exp, dtype=jnp.int32)[None, :]).astype(jnp.int32)
    pair_rank = jnp.sum((jnp.cumsum(onehot, axis=0) - onehot) * onehot, axis=1)
    pair_copies = exp_copies[flat_exp]
    slot_flat = slot_of[flat_exp, pair_rank % pair_copies]
    buf_row = pair_rank // pair_copies
    pair_pos = ((slot_flat % n_slot) * n_dev + slot_flat // n_slot) * capacity + buf_row
    pair_tok = jnp.arange(flat_exp.shape[0], dtype=jnp.int32) // n_top
    buf_tok = jnp.zeros((n_slot * n_dev * capacity,), jnp.int32).at[pair_pos].set(pair_tok)
    return pair_pos, buf_tok


def expert_ffn(recv_buf, up_local, down_local):
    pre_act = jnp.einsum('spcm,smf->spcf', recv_buf, up_local, preferred_element_type=jnp.float32)
    hidden = jax.nn.gelu(pre_act, approximate=True).astype(jnp.bfloat16)
    return jnp.einsum('spcf,sfm->spcm', hidden, down_local, preferred_element_type=jnp.float32).astype(jnp.bfloat16)


def general_layer(tokens, topk_idx, topk_w, w_up, w_down, slot_expert):
    n_tok, d_model = tokens.shape
    n_top = topk_idx.shape[1]
    n_dev, n_slot = slot_expert.shape
    capacity = slot_bound(n_tok, n_top, n_dev, n_slot)
    pair_pos, buf_tok = route_pairs(topk_idx, slot_expert, capacity)
    send_buf = tokens[buf_tok].reshape(n_slot, n_dev, capacity, d_model)
    recv_buf = lax.all_to_all(send_buf, 'ep', 1, 1, tiled=True)
    expert_out = expert_ffn(recv_buf, w_up[0], w_down[0])
    back_buf = lax.all_to_all(expert_out, 'ep', 1, 1, tiled=True)
    pair_out = back_buf.reshape(-1, d_model)[pair_pos]
    return (pair_out.astype(jnp.float32) * topk_w).astype(jnp.bfloat16)


def chunk_rows(k):
    return SEND_AT[k + 1] - SEND_AT[k], BACK_AT[k + 1] - BACK_AT[k]


def stream_starts(counts, hot_slot):
    out_at, back_at = [], []
    out_end = back_end = jnp.zeros_like(counts[0])
    for s, count in enumerate(counts):
        out_at.append(out_end)
        floor = jnp.where(hot_slot < s, float(BACK_AT[max(s - 1, 0)]), float(BACK_AT[min(s, N_SEG - 1)]))
        start = jnp.where(hot_slot == s, back_end, jnp.maximum(back_end, floor))
        back_at.append(start)
        out_end = out_end + count
        back_end = start + count
    return out_at, back_at, out_end


def route(idx_row, table, peers, n_exp, n_slot):
    f32 = jnp.float32
    n_tok = idx_row.shape[1]
    lanes = 128
    onehot = (lax.broadcasted_iota(jnp.int32, (n_exp, n_tok), 0) == idx_row).astype(f32)
    step = 256
    blocks = [onehot[:, b * step:(b + 1) * step] for b in range(n_tok // step)]
    before = lax.broadcasted_iota(jnp.int32, (step, step), 0) < lax.broadcasted_iota(jnp.int32, (step, step), 1)
    local_rank = jnp.dot(jnp.concatenate(blocks, axis=0).astype(jnp.bfloat16), before.astype(f32).astype(jnp.bfloat16), preferred_element_type=f32)
    carry = jnp.zeros((n_exp, 1), f32)
    ranks = []
    for b, block in enumerate(blocks):
        ranks.append(local_rank[b * n_exp:(b + 1) * n_exp] + carry)
        carry = carry + jnp.sum(block, axis=1, keepdims=True)
    rank = jnp.concatenate(ranks, axis=1)
    n_pair = jnp.broadcast_to(carry, (n_exp, lanes))

    exp_id = lax.broadcasted_iota(jnp.int32, (n_exp, lanes), 0)
    match = [[(exp_id == table[d, s]).astype(f32) for s in range(n_slot)] for d in peers]
    copies = sum(sum(row) for row in match)
    per_copy = 1.0 / copies
    hot = (copies == 4.0).astype(f32)
    own = sum(match[0])
    own_slot = sum(s * match[0][s] for s in range(n_slot))
    seen = jnp.zeros((n_exp, lanes), f32)
    start_out = [jnp.zeros((n_exp, lanes), f32) for _ in range(MAX_COPIES)]
    start_back = [jnp.zeros((n_exp, lanes), f32) for _ in range(MAX_COPIES)]
    total = jnp.zeros((1, lanes), f32)
    stream_counts = []
    for r in range(len(peers)):
        seens, counts = [], []
        peer_hot = jnp.zeros((1, lanes), f32)
        for s in range(n_slot):
            here = match[r][s]
            seens.append(seen)
            rows = jnp.floor((n_pair - seen + copies - 0.5) * per_copy)
            counts.append(jnp.sum(here * (1.0 - own) * rows, axis=0, keepdims=True))
            peer_hot = peer_hot + s * jnp.sum(here * hot, axis=0, keepdims=True)
            seen = seen + here
        out_at, back_at, end = stream_starts(counts, peer_hot)
        if r == 0:
            hot_slot = peer_hot
        if r >= 2:
            stream_counts.append(counts)
            total = jnp.maximum(total, end)
        for s in range(n_slot):
            local = LOCAL_BASE + SLOT_ROWS * own_slot + SEG * r
            if r == 0:
                code_out = code_back = local
            elif r == 1:
                seg = s - (peer_hot < s).astype(f32)
                code_out = code_back = jnp.where(own > 0, local, STREAM_AT[1] + SEG * seg)
            else:
                code_out = jnp.where(own > 0, local, STREAM_AT[r] + out_at[s])
                code_back = jnp.where(own > 0, local, STREAM_AT[r] + back_at[s])
            for c in range(MAX_COPIES):
                mine = (match[r][s] > 0) & (seens[s] == c)
                start_out[c] = jnp.where(mine, code_out, start_out[c])
                start_back[c] = jnp.where(mine, code_back, start_back[c])

    wide = lambda a: jnp.concatenate([a] * (n_tok // lanes), axis=1)
    row = jnp.floor((rank + 0.5) * wide(per_copy))
    which = rank - row * wide(copies)
    codes = []
    for starts in (start_out, start_back):
        start = wide(starts[3])
        for c in range(MAX_COPIES - 1):
            start = jnp.where(which == c, wide(starts[c]), start)
        codes.append(jnp.sum(onehot * (start + row), axis=0, keepdims=True).astype(jnp.int32))
    fits = jnp.max(own * hot, axis=0, keepdims=True) * (total <= PAIR).astype(f32)
    return codes, hot_slot, stream_counts, fits


def layer_kernel(slot_expert, topk_idx, topk_w, tokens, w_up, w_down, out, last_rows, last_mask, last_gate, found, table, idx_row, gate_row, tok_buf, up_buf, down_buf, send_core, recv_core, send_chip, recv_chip, acc, rows_buf, back_core, back_chip, early, mixed, mask_buf, gate_buf, code_row, back_row, code_col, gate_col, counts_out, counts_in, flags, t_sem, w_sem, ds_sem, dr_sem, bs_sem, br_sem, o_sem, cs_sem, cr_sem, fs_sem, fr_sem):
    f32, bf16 = jnp.float32, jnp.bfloat16
    n_tok, d_model = tok_buf.shape
    n_slot = w_up.shape[0]
    d_ff = w_up.shape[2]
    me = lax.axis_index('ep')
    group = lax.axis_index('dp')
    chip, core = me // 2, me % 2
    peers = [me, 2 * chip + (1 - core), 2 * (1 - chip) + core, 2 * (1 - chip) + (1 - core)]
    peer_ids = [None] + [{'ep': peers[r]} for r in (1, 2, 3)] + [{'dp': 1 - group}]

    barrier = pltpu.get_barrier_semaphore()
    for r in (1, 2, 3, 4):
        pl.semaphore_signal(barrier, inc=1, device_id=peer_ids[r], device_id_type=MESH)

    def weight_copies(s):
        b = s % N_WBUF
        return (pltpu.make_async_copy(w_up.at[s], up_buf.at[b], w_sem.at[s, 0]),
                pltpu.make_async_copy(w_down.at[s], down_buf.at[b], w_sem.at[s, 1]))

    small_copies = [pltpu.make_async_copy(slot_expert, table, t_sem.at[0]),
                    pltpu.make_async_copy(topk_idx, idx_row, t_sem.at[1]),
                    pltpu.make_async_copy(topk_w, gate_row, t_sem.at[2])]
    token_copy = pltpu.make_async_copy(tokens, tok_buf, t_sem.at[3])
    for copy in small_copies:
        copy.start()
    token_copy.start()
    for copy in small_copies:
        copy.wait()
    (code_out, code_back), hot_slot, stream_counts, fits = route(idx_row[...], table, peers, 16, n_slot)
    code_row[...] = jnp.broadcast_to(code_out, code_row.shape)
    back_row[...] = jnp.broadcast_to(code_back, back_row.shape)
    hot_slot = hot_slot[:, :1]
    for r in (2, 3):
        counts_out[r - 2] = jnp.concatenate(stream_counts[r - 2] + [jnp.zeros((8 - n_slot, 128), f32)], axis=0)
    flags[0] = jnp.broadcast_to(fits, (8, 128))

    def pick(ids):
        mask = (ids == code_row[0:1, :]).astype(f32).astype(bf16)
        return jnp.dot(mask, tok_buf[...], preferred_element_type=f32).astype(bf16)

    def ids_from(first, rows):
        return lax.broadcasted_iota(jnp.int32, (rows, n_tok), 0) + first

    def dispatch_copy(k, r):
        if r == 1:
            rows = pl.ds(k * SEG, SEG)
            src, dst = send_core.at[rows], recv_core.at[rows]
        else:
            rows = pl.ds(SEND_AT[k], chunk_rows(k)[0])
            src, dst = send_chip.at[r - 2, rows], recv_chip.at[r - 2, rows]
        return pltpu.make_async_remote_copy(
            src_ref=src, dst_ref=dst, send_sem=ds_sem.at[k, r - 1], recv_sem=dr_sem.at[k, r - 1],
            device_id=peer_ids[r], device_id_type=MESH)

    def back_copy(k, r):
        size = chunk_rows(k)[1]
        if r == 1:
            src, to_early, to_last = back_core.at[pl.ds(k * SEG, SEG)], pl.ds(k * SEG, SEG), pl.ds(0, SEG)
        else:
            src = back_chip.at[r - 2, pl.ds(BACK_AT[k], size)]
            to_early = pl.ds(3 * SEG + (r - 2) * BACK_AT[3] + BACK_AT[k], size)
            to_last = pl.ds((r - 1) * SEG, SEG)
        return pltpu.make_async_remote_copy(
            src_ref=src, dst_ref=early.at[to_early] if k < N_SEG - 1 else last_rows.at[to_last],
            send_sem=bs_sem.at[k, r - 1], recv_sem=br_sem.at[k, r - 1],
            device_id=peer_ids[r], device_id_type=MESH)

    def counts_copy(r):
        return pltpu.make_async_remote_copy(
            src_ref=counts_out.at[r - 2], dst_ref=counts_in.at[r - 2], send_sem=cs_sem.at[r - 2], recv_sem=cr_sem.at[r - 2],
            device_id=peer_ids[r], device_id_type=MESH)

    def flag_copy(r):
        src, dst = (0, 1) if r == 4 else (2, 2 + r)
        return pltpu.make_async_remote_copy(
            src_ref=flags.at[src], dst_ref=flags.at[dst], send_sem=fs_sem.at[r - 1], recv_sem=fr_sem.at[r - 1],
            device_id=peer_ids[r], device_id_type=MESH)

    token_copy.wait()
    for s in range(N_WBUF):
        for copy in weight_copies(s):
            copy.start()
    for k in range(N_SEG):
        size = chunk_rows(k)[0]
        ids = [ids_from(STREAM_AT[2] + SEND_AT[k], size), ids_from(STREAM_AT[3] + SEND_AT[k], size), ids_from(k * SEG, SEG)]
        picked = pick(jnp.concatenate(ids, axis=0))
        send_chip[0, SEND_AT[k]:SEND_AT[k + 1], :] = picked[:size]
        send_chip[1, SEND_AT[k]:SEND_AT[k + 1], :] = picked[size:2 * size]
        send_core[k * SEG:(k + 1) * SEG, :] = picked[2 * size:]
        if k == 0:
            pl.semaphore_wait(barrier, 4)
            for r in (2, 3):
                counts_copy(r).start()
        for r in (2, 3, 1):
            dispatch_copy(k, r).start()
    flag_copy(4).start()

    for s in range(n_slot):
        rows_buf[s * SLOT_ROWS:(s + 1) * SLOT_ROWS, :] = pick(ids_from(LOCAL_BASE + s * SLOT_ROWS, SLOT_ROWS))
    code_col[...] = jnp.transpose(jnp.broadcast_to(code_back, (128, n_tok)))
    gate_col[...] = jnp.transpose(jnp.broadcast_to(gate_row[...], (128, n_tok)))
    n_early = 3 * SEG + 2 * BACK_AT[3]
    early[n_early:, :] = jnp.zeros((EARLY_ROWS - n_early, d_model), bf16)
    rows_buf[n_slot * SLOT_ROWS:, :] = jnp.zeros((LOCAL_ROWS - n_slot * SLOT_ROWS, d_model), bf16)

    def last_ids(i):
        core_id = STREAM_AT[1] + 3 * SEG + i
        chip_id = jnp.where(i < 2 * SEG, STREAM_AT[2] + BACK_AT[3] - SEG, STREAM_AT[3] + BACK_AT[3] - 2 * SEG) + i
        return jnp.where(i < SEG, core_id, jnp.where(i < 3 * SEG, chip_id, -1))

    def early_ids(i):
        chip_id = jnp.where(i < 3 * SEG + BACK_AT[3], STREAM_AT[2] - 3 * SEG, STREAM_AT[3] - 3 * SEG - BACK_AT[3]) + i
        return jnp.where(i < 3 * SEG, STREAM_AT[1] + i, jnp.where(i < n_early, chip_id, -1))

    ids = last_ids(lax.broadcasted_iota(jnp.int32, (3 * SEG, n_tok), 0))
    gates = jnp.sum(jnp.where(ids == back_row[0:1, :], gate_row[...], 0.0), axis=1, keepdims=True)
    gate_buf[...] = jnp.broadcast_to(gates, gate_buf.shape)
    lane = lax.broadcasted_iota(jnp.int32, (n_tok, 128), 1)
    for j in range(LAST_ROWS // 128):
        mask_buf[:, j * 128:(j + 1) * 128] = (code_col[...] == last_ids(lane + 128 * j)).astype(f32).astype(bf16)
    side_copies = [pltpu.make_async_copy(mask_buf, last_mask, t_sem.at[4]),
                   pltpu.make_async_copy(gate_buf, last_gate, t_sem.at[5])]
    for copy in side_copies:
        copy.start()
    flag_copy(4).wait_recv()
    flags[2] = jnp.minimum(flags[0], flags[1])
    for r in (1, 2, 3):
        flag_copy(r).start()
    for r in (2, 3):
        counts_copy(r).wait_recv()
    in_counts = [[counts_in[j, s:s + 1, :1] for s in range(n_slot)] for j in range(2)]
    in_starts = [stream_starts(counts, hot_slot) for counts in in_counts]
    as_int = lambda a: a.astype(jnp.int32)

    for s in range(n_slot):
        lo, hi = s * SLOT_ROWS, (s + 1) * SLOT_ROWS
        if s < N_SEG:
            for r in (1, 2, 3):
                dispatch_copy(s, r).wait_recv()
        near = rows_buf[lo + SEG:lo + 2 * SEG, :].astype(f32)
        if s < N_SEG:
            near = near + recv_core[s * SEG:(s + 1) * SEG, :].astype(f32) * (hot_slot > s).astype(f32)
        if s > 0:
            near = near + recv_core[(s - 1) * SEG:s * SEG, :].astype(f32) * (hot_slot < s).astype(f32)
        rows_buf[lo + SEG:lo + 2 * SEG, :] = near.astype(bf16)
        come = SEND_AT[min(s, N_SEG - 1) + 1]
        i = lax.broadcasted_iota(jnp.int32, (SEG, come), 0)
        j = lax.broadcasted_iota(jnp.int32, (SEG, come), 1)
        for r in (2, 3):
            mask = (j - i == as_int(in_starts[r - 2][0][s])) & (i < as_int(in_counts[r - 2][s]))
            far = jnp.dot(mask.astype(f32).astype(bf16), recv_chip[r - 2, :come, :], preferred_element_type=f32)
            at = slice(lo + r * SEG, lo + (r + 1) * SEG)
            rows_buf[at, :] = (rows_buf[at, :].astype(f32) + far).astype(bf16)
        for copy in weight_copies(s):
            copy.wait()
        b = s % N_WBUF
        acc[...] = jnp.zeros_like(acc)

        def ff_step(i, carry):
            cols = pl.ds(pl.multiple_of(i * FF_TILE, FF_TILE), FF_TILE)
            pre = jnp.dot(rows_buf[lo:hi, :], up_buf[b, :, cols], preferred_element_type=f32)
            hidden = jax.nn.gelu(pre, approximate=True).astype(bf16)
            acc[...] += jnp.dot(hidden, down_buf[b, cols, :], preferred_element_type=f32)
            return carry

        lax.fori_loop(0, d_ff // FF_TILE, ff_step, 0)
        if s + N_WBUF < n_slot:
            for copy in weight_copies(s + N_WBUF):
                copy.start()
        rows_buf[lo:hi, :] = acc[...].astype(bf16)
        if s > 0:
            k = s - 1
            size = chunk_rows(k)[1]
            slots = list(range(max(k - 1, 0), s + 1))
            i = lax.broadcasted_iota(jnp.int32, (size, SEG * len(slots)), 0)
            j = lax.broadcasted_iota(jnp.int32, (size, SEG * len(slots)), 1)
            for r in (2, 3):
                mask = jnp.zeros(i.shape, f32)
                for n, q in enumerate(slots):
                    row = j - n * SEG
                    fit = (i + BACK_AT[k] - row == as_int(in_starts[r - 2][1][q])) & (row >= 0) & (row < as_int(in_counts[r - 2][q]))
                    mask = jnp.where(fit, 1.0, mask)
                done = jnp.concatenate([rows_buf[q * SLOT_ROWS + r * SEG:q * SLOT_ROWS + (r + 1) * SEG, :] for q in slots], axis=0)
                back_chip[r - 2, BACK_AT[k]:BACK_AT[k + 1], :] = jnp.dot(mask.astype(bf16), done, preferred_element_type=f32).astype(bf16)
                back_copy(k, r).start()
            prev = rows_buf[lo - SLOT_ROWS + SEG:lo - SLOT_ROWS + 2 * SEG, :].astype(f32)
            last = rows_buf[lo + SEG:lo + 2 * SEG, :].astype(f32)
            back = prev * (hot_slot > k).astype(f32) + last * (hot_slot <= k).astype(f32)
            back_core[k * SEG:(k + 1) * SEG, :] = back.astype(bf16)
            back_copy(k, 1).start()

    tile = 256
    n_tile = n_tok // tile

    def out_copy(i):
        at = pl.ds(pl.multiple_of(i * tile, tile), tile)
        return pltpu.make_async_copy(mixed.at[at], out.at[at], o_sem.at[i])

    def combine(ids_of, rows, source, final):
        def body(i, carry):
            at = pl.ds(pl.multiple_of(i * tile, tile), tile)
            mine = code_col[at, :]
            lane = lax.broadcasted_iota(jnp.int32, (tile, 128), 1)
            mask = jnp.concatenate([(mine == ids_of(lane + 128 * j)).astype(f32).astype(bf16) for j in range(rows // 128)], axis=1)
            part = jnp.dot(mask, source[...], preferred_element_type=f32)
            if final:
                part = part + mixed[at, :].astype(f32)
                part = part * jnp.concatenate([gate_col[at, :]] * (d_model // 128), axis=1)
            mixed[at, :] = part.astype(bf16)
            if final:
                out_copy(i).start()
            return carry
        lax.fori_loop(0, n_tile, body, 0)

    combine(lambda i: LOCAL_BASE + i, LOCAL_ROWS, rows_buf, False)
    for r in (1, 2, 3):
        flag_copy(r).wait_recv()
    agreed = jnp.minimum(jnp.minimum(flags[2], flags[3]), jnp.minimum(flags[4], flags[5]))
    found[...] = agreed[0:1, :].astype(jnp.int32)
    for k in range(N_SEG):
        for r in (1, 2, 3):
            back_copy(k, r).wait_recv()
        if k == N_SEG - 2:
            combine(early_ids, EARLY_ROWS, early, True)
            for i in range(n_tile):
                out_copy(i).wait()
            for copy in side_copies:
                copy.wait()
    for r in (2, 3):
        counts_copy(r).wait_send()
    for r in (1, 2, 3, 4):
        flag_copy(r).wait_send()
    for k in range(N_SEG):
        for r in (1, 2, 3):
            dispatch_copy(k, r).wait_send()
            back_copy(k, r).wait_send()


def last_kernel(part, rows, mask, gate, out):
    f32, bf16 = jnp.float32, jnp.bfloat16
    d_model = part.shape[1]
    gates = jnp.concatenate([gate[...]] * (d_model // 128), axis=1)
    scaled = (rows[...].astype(f32) * gates).astype(bf16)
    scaled = jnp.concatenate([scaled, jnp.zeros((LAST_ROWS - scaled.shape[0], d_model), bf16)], axis=0)
    late = jnp.dot(mask[...], scaled, preferred_element_type=f32)
    out[...] = (late + part[...].astype(f32)).astype(bf16)


def add_last(part, rows, mask, gate):
    n_tok, d_model = part.shape
    tile = 512
    by_tile = lambda cols: pl.BlockSpec((tile, cols), lambda i: (i, 0))
    whole = lambda a: pl.BlockSpec(a.shape, lambda i: (0, 0))
    return pl.pallas_call(
        last_kernel,
        grid=(n_tok // tile,),
        out_shape=jax.ShapeDtypeStruct(part.shape, part.dtype),
        in_specs=[by_tile(d_model), whole(rows), by_tile(mask.shape[1]), whole(gate)],
        out_specs=by_tile(d_model),
    )(part, rows, mask, gate)


def fast_layer(tokens, topk_idx, topk_w, w_up, w_down, slot_expert):
    n_tok, d_model = tokens.shape
    n_slot, d_ff = w_up.shape[1], w_up.shape[3]
    vmem = pl.BlockSpec(memory_space=pltpu.VMEM)
    anym = pl.BlockSpec(memory_space=pl.ANY)
    bf16, f32 = jnp.bfloat16, jnp.float32
    shape = jax.ShapeDtypeStruct
    dma = pltpu.SemaphoreType.DMA
    return pl.pallas_call(
        layer_kernel,
        out_shape=(shape((n_tok, d_model), bf16), shape((3 * SEG, d_model), bf16), shape((n_tok, LAST_ROWS), bf16),
                   shape((3 * SEG, 128), f32), shape((1, 128), jnp.int32)),
        in_specs=[anym] * 6,
        out_specs=(anym, anym, anym, anym, vmem),
        scratch_shapes=[
            pltpu.SMEM(slot_expert.shape, jnp.int32),
            pltpu.VMEM((1, n_tok), jnp.int32),
            pltpu.VMEM((1, n_tok), f32),
            pltpu.VMEM((n_tok, d_model), bf16),
            pltpu.VMEM((N_WBUF, d_model, d_ff), bf16),
            pltpu.VMEM((N_WBUF, d_ff, d_model), bf16),
            pltpu.VMEM((N_SEG * SEG, d_model), bf16),
            pltpu.VMEM((N_SEG * SEG, d_model), bf16),
            pltpu.VMEM((2, PAIR, d_model), bf16),
            pltpu.VMEM((2, PAIR, d_model), bf16),
            pltpu.VMEM((SLOT_ROWS, d_model), f32),
            pltpu.VMEM((LOCAL_ROWS, d_model), bf16),
            pltpu.VMEM((N_SEG * SEG, d_model), bf16),
            pltpu.VMEM((2, PAIR, d_model), bf16),
            pltpu.VMEM((EARLY_ROWS, d_model), bf16),
            pltpu.VMEM((n_tok, d_model), bf16),
            pltpu.VMEM((n_tok, LAST_ROWS), bf16),
            pltpu.VMEM((3 * SEG, 128), f32),
            pltpu.VMEM((8, n_tok), jnp.int32),
            pltpu.VMEM((8, n_tok), jnp.int32),
            pltpu.VMEM((n_tok, 128), jnp.int32),
            pltpu.VMEM((n_tok, 128), f32),
            pltpu.VMEM((2, 8, 128), f32),
            pltpu.VMEM((2, 8, 128), f32),
            pltpu.VMEM((6, 8, 128), f32),
            dma((6,)), dma((n_slot, 2)),
            dma((N_SEG, 3)), dma((N_SEG, 3)), dma((N_SEG, 3)), dma((N_SEG, 3)),
            dma((n_tok // 256,)), dma((2,)), dma((2,)), dma((4,)), dma((4,)),
        ],
        compiler_params=pltpu.CompilerParams(collective_id=0, has_side_effects=True, vmem_limit_bytes=60 * 1024 * 1024),
    )(slot_expert, topk_idx.reshape(1, n_tok), topk_w.reshape(1, n_tok), tokens, w_up[0], w_down[0])


def solution(mesh):
    def group_layer(tokens, topk_idx, topk_w, w_up, w_down, slot_expert):
        *parts, found = fast_layer(tokens, topk_idx, topk_w, w_up, w_down, slot_expert)
        args = (*parts, tokens, topk_idx, topk_w, w_up, w_down, slot_expert)
        return lax.cond(found[0, 0] == 1, lambda *a: add_last(*a[:4]), lambda *a: general_layer(*a[4:]), *args)

    row_spec = P(('dp', 'ep'), None)
    weight_spec = P('ep', None, None, None)
    return jax.shard_map(group_layer, mesh=mesh, in_specs=(row_spec, row_spec, row_spec, weight_spec, weight_spec, P(None, None)), out_specs=row_spec, check_vma=False)
```

time: 53.7 us -> 52.6 us (0.980)
  Pallas kernels: 51.6 us -> 50.5 us
    pallas_call x1, Pallas kernels: 2.87 us -> 1.93 us  [add_last(): pl.pallas_call(last_kernel, grid=(n_tok // tile,), out_shape=jax.ShapeDty...]
where the time goes in v4:
time: 52.6 us; the launch traced here: 52.4 us
  Pallas kernels  50.5 us (96%)
  local copies, waits for them, and re-layouts  1.15 us (2%)
  between operations  0.75 us (1%)
    pallas_call x1, Pallas kernels, fast_layer(): pl.pallas_call(layer_kernel, out_shape=(shape((n_tok, d_model), bf16), sh...  48.6 us
    pallas_call x1, Pallas kernels, add_last(): pl.pallas_call(last_kernel, grid=(n_tok // tile,), out_shape=jax.ShapeDty...  1.93 us
    unnamed x10, local copies, waits for them, and re-layouts  1.15 us

profile of v4, /device:TPU:0, one launch (start us, length us, event | category | flops | bytes accessed | tf_op | source)
XLA Modules:
  0.0 52.4 jit_solution(230304286708570204)
XLA Ops:
  0.0 0.0 copy-start
  0.0 0.0 copy-start.2
  0.0 0.0 copy-start.3
  0.0 0.0 copy-start.4
  0.0 48.6 %shard_map.66 = (bf16[1024,768]{1,0:T(8,128)(2,1)}, bf16[240,768]{1,0:T(8,128)(2,1)S(1)}, bf16[1024,256]{1,0:T(8,128)(2,1)S(1)}, f32[240,128]{1,0:T(8,128)S(1)}, s32[1,128]{1,0:T(1,128)}) custom-call(s32[4,5]{1,0:T(4,128)} %slot_expert.1, s32[1,1024]{1,0:T(1,128)} %bitcast.76, f32[1,1024]{1,0:T(1,128)} %bitcast.83, bf16[1024,768]{1,0:T(8,128)(2,1)} %tokens.1, ...), custom_call_target="tpu_custom_call" | custom-call | tf_op jit(solution)/shard_map/pallas_call | solution.py:436
  49.3 0.0 copy-done
  49.3 0.0 copy-done.2
  49.3 0.0 copy-done.3
  49.3 0.0 copy-done.4
  49.3 2.0 %conditional.1 = (bf16[1024,768]{1,0:T(8,128)(2,1)S(1)}) conditional(s32[]{:T(128)} %bitcast.40, (s32[4,5]{1,0:T(4,128)S(1)}, s32[1024,1]{0,1:T(1,128)S(1)}, bf16[1024,768]{1,0:T(8,128)(2,1)S(1)}, bf16[1,5,768,3072]{3,2,1,0:T(8,128)(2,1)}, bf16[1,5,3072,768]{3,2,1,0:T(8,128)(2,1)}, /*index=5*/f32[1024,1]{0,1:T(1,128)S(1)}) %tuple.46, ...), branch_computations={%region_0.8_spmd, %region_8.9_spmd} | conditional | flops 14581685248 | bytes 137039296 | solution.py:480
  49.3 1.9 %branch_1_fun.1 = bf16[1024,768]{1,0:T(8,128)(2,1)S(1)} custom-call(bf16[1024,768]{1,0:T(8,128)(2,1)} %get-tuple-element.34.part, bf16[240,768]{1,0:T(8,128)(2,1)S(1)} %get-tuple-element.35.rows, bf16[1024,256]{1,0:T(8,128)(2,1)S(1)} %get-tuple-element.36.mask, f32[240,128]{1,0:T(8,128)S(1)} %get-tuple-element.37.gate), custom_call_target="tpu_custom_call" | custom-call | tf_op jit(solution)/shard_map/cond/branch_1_fun/pallas_call | solution.py:419
  51.3 0.0 copy-start.1
  51.3 1.1 %copy-done.1 = bf16[1024,768]{1,0:T(8,128)(2,1)} copy-done((bf16[1024,768]{1,0:T(8,128)(2,1)}, bf16[1024,768]{1,0:T(8,128)(2,1)S(1)}, u32[]{:S(2)}) %copy-start.1) | copy-done | bytes 1572888
Async XLA Ops:
  0.0 49.3 %copy-start = (bf16[1024,768]{1,0:T(8,128)(2,1)S(1)}, bf16[1024,768]{1,0:T(8,128)(2,1)}, u32[]{:S(2)}) copy-start(bf16[1024,768]{1,0:T(8,128)(2,1)} %tokens.1) | copy-start | bytes 4718596
  0.0 49.3 %copy-start.2 = (s32[1024,1]{0,1:T(1,128)S(1)}, s32[1024,1]{0,1:T(1,128)}, u32[]{:S(2)}) copy-start(s32[1024,1]{0,1:T(1,128)} %param.9) | copy-start | bytes 12292
  0.0 49.3 %copy-start.3 = (s32[4,5]{1,0:T(4,128)S(1)}, s32[4,5]{1,0:T(4,128)}, u32[]{:S(2)}) copy-start(s32[4,5]{1,0:T(4,128)} %slot_expert.1) | copy-start | bytes 244
  0.0 49.3 %copy-start.4 = (f32[1024,1]{0,1:T(1,128)S(1)}, f32[1024,1]{0,1:T(1,128)}, u32[]{:S(2)}) copy-start(f32[1024,1]{0,1:T(1,128)} %param.10) | copy-start | bytes 12292
  51.3 1.1 %copy-start.1 = (bf16[1024,768]{1,0:T(8,128)(2,1)}, bf16[1024,768]{1,0:T(8,128)(2,1)S(1)}, u32[]{:S(2)}) copy-start(bf16[1024,768]{1,0:T(8,128)(2,1)S(1)} %get-tuple-element.83) | copy-start | bytes 4718596

commit v5 on v4

--- a/solution.py
+++ b/solution.py
@@ -19,7 +19,7 @@
 LOCAL_ROWS = 1664
 LAST_ROWS = 256
 EARLY_ROWS = 768
-FF_TILE = 512
+FF_TILE = 1536
 N_WBUF = 4
 MESH = pl.DeviceIdType.MESH
 

time: 52.6 us -> 49.2 us (0.935)
  Pallas kernels: 50.5 us -> 47.2 us
    pallas_call x1, Pallas kernels: 48.6 us -> 45.3 us  [fast_layer(): pl.pallas_call(layer_kernel, out_shape=(shape((n_tok, d_model), bf16), sh...]
where the time goes in v5:
time: 49.2 us; the launch traced here: 49.1 us
  Pallas kernels  47.2 us (96%)
  local copies, waits for them, and re-layouts  1.15 us (2%)
  between operations  0.75 us (2%)
    pallas_call x1, Pallas kernels, fast_layer(): pl.pallas_call(layer_kernel, out_shape=(shape((n_tok, d_model), bf16), sh...  45.3 us
    pallas_call x1, Pallas kernels, add_last(): pl.pallas_call(last_kernel, grid=(n_tok // tile,), out_shape=jax.ShapeDty...  1.92 us
    unnamed x10, local copies, waits for them, and re-layouts  1.15 us

profile of v5, /device:TPU:0, one launch (start us, length us, event | category | flops | bytes accessed | tf_op | source)
XLA Modules:
  0.0 49.1 jit_solution(1506048421608582730)
XLA Ops:
  0.0 0.0 copy-start
  0.0 0.0 copy-start.2
  0.0 0.0 copy-start.3
  0.0 0.0 copy-start.4
  0.0 45.3 %shard_map.66 = (bf16[1024,768]{1,0:T(8,128)(2,1)}, bf16[240,768]{1,0:T(8,128)(2,1)S(1)}, bf16[1024,256]{1,0:T(8,128)(2,1)S(1)}, f32[240,128]{1,0:T(8,128)S(1)}, s32[1,128]{1,0:T(1,128)}) custom-call(s32[4,5]{1,0:T(4,128)} %slot_expert.1, s32[1,1024]{1,0:T(1,128)} %bitcast.76, f32[1,1024]{1,0:T(1,128)} %bitcast.83, bf16[1024,768]{1,0:T(8,128)(2,1)} %tokens.1, ...), custom_call_target="tpu_custom_call" | custom-call | tf_op jit(solution)/shard_map/pallas_call | solution.py:436
  46.0 0.0 copy-done
  46.0 0.0 copy-done.2
  46.0 0.0 copy-done.3
  46.0 0.0 copy-done.4
  46.0 1.9 %conditional.1 = (bf16[1024,768]{1,0:T(8,128)(2,1)S(1)}) conditional(s32[]{:T(128)} %bitcast.40, (s32[4,5]{1,0:T(4,128)S(1)}, s32[1024,1]{0,1:T(1,128)S(1)}, bf16[1024,768]{1,0:T(8,128)(2,1)S(1)}, bf16[1,5,768,3072]{3,2,1,0:T(8,128)(2,1)}, bf16[1,5,3072,768]{3,2,1,0:T(8,128)(2,1)}, /*index=5*/f32[1024,1]{0,1:T(1,128)S(1)}) %tuple.46, ...), branch_computations={%region_0.8_spmd, %region_8.9_spmd} | conditional | flops 14581685248 | bytes 137039296 | solution.py:480
  46.0 1.9 %branch_1_fun.1 = bf16[1024,768]{1,0:T(8,128)(2,1)S(1)} custom-call(bf16[1024,768]{1,0:T(8,128)(2,1)} %get-tuple-element.34.part, bf16[240,768]{1,0:T(8,128)(2,1)S(1)} %get-tuple-element.35.rows, bf16[1024,256]{1,0:T(8,128)(2,1)S(1)} %get-tuple-element.36.mask, f32[240,128]{1,0:T(8,128)S(1)} %get-tuple-element.37.gate), custom_call_target="tpu_custom_call" | custom-call | tf_op jit(solution)/shard_map/cond/branch_1_fun/pallas_call | solution.py:419
  48.0 0.0 copy-start.1
  48.0 1.1 %copy-done.1 = bf16[1024,768]{1,0:T(8,128)(2,1)} copy-done((bf16[1024,768]{1,0:T(8,128)(2,1)}, bf16[1024,768]{1,0:T(8,128)(2,1)S(1)}, u32[]{:S(2)}) %copy-start.1) | copy-done | bytes 1572888
Async XLA Ops:
  0.0 46.0 %copy-start = (bf16[1024,768]{1,0:T(8,128)(2,1)S(1)}, bf16[1024,768]{1,0:T(8,128)(2,1)}, u32[]{:S(2)}) copy-start(bf16[1024,768]{1,0:T(8,128)(2,1)} %tokens.1) | copy-start | bytes 4718596
  0.0 46.0 %copy-start.2 = (s32[1024,1]{0,1:T(1,128)S(1)}, s32[1024,1]{0,1:T(1,128)}, u32[]{:S(2)}) copy-start(s32[1024,1]{0,1:T(1,128)} %param.9) | copy-start | bytes 12292
  0.0 46.0 %copy-start.3 = (s32[4,5]{1,0:T(4,128)S(1)}, s32[4,5]{1,0:T(4,128)}, u32[]{:S(2)}) copy-start(s32[4,5]{1,0:T(4,128)} %slot_expert.1) | copy-start | bytes 244
  0.0 46.0 %copy-start.4 = (f32[1024,1]{0,1:T(1,128)S(1)}, f32[1024,1]{0,1:T(1,128)}, u32[]{:S(2)}) copy-start(f32[1024,1]{0,1:T(1,128)} %param.10) | copy-start | bytes 12292
  48.0 1.1 %copy-start.1 = (bf16[1024,768]{1,0:T(8,128)(2,1)}, bf16[1024,768]{1,0:T(8,128)(2,1)S(1)}, u32[]{:S(2)}) copy-start(bf16[1024,768]{1,0:T(8,128)(2,1)S(1)} %get-tuple-element.83) | copy-start | bytes 4718596

commit v6 on v5

--- a/solution.py
+++ b/solution.py
@@ -10,15 +10,18 @@
 MAX_COPIES = 4
 SEG = 80
 N_SEG = 4
-PAIR = 288
-SEND_AT = (0, 80, 160, 240, 288)
-BACK_AT = (0, 48, 128, 208, 288)
+DIRECT = 240
+SHARED = 64
+SEND_AT = (0, 80, 160, 240)
+BACK_AT = (0, 48, 112, 192, 240)
 SLOT_ROWS = 4 * SEG
-STREAM_AT = (None, 0, N_SEG * SEG, N_SEG * SEG + PAIR)
+STREAM_AT = (None, 0, N_SEG * SEG, N_SEG * SEG + DIRECT)
+SHARED_AT = N_SEG * SEG + 2 * DIRECT
+RAW_AT = (None, None, 4096, 6144)
 LOCAL_BASE = 1024
 LOCAL_ROWS = 1664
 LAST_ROWS = 256
-EARLY_ROWS = 768
+EARLY_ROWS = 640
 FF_TILE = 1536
 N_WBUF = 4
 MESH = pl.DeviceIdType.MESH
@@ -72,10 +75,6 @@
     return (pair_out.astype(jnp.float32) * topk_w).astype(jnp.bfloat16)
 
 
-def chunk_rows(k):
-    return SEND_AT[k + 1] - SEND_AT[k], BACK_AT[k + 1] - BACK_AT[k]
-
-
 def stream_starts(counts, hot_slot):
     out_at, back_at = [], []
     out_end = back_end = jnp.zeros_like(counts[0])
@@ -86,7 +85,7 @@
         back_at.append(start)
         out_end = out_end + count
         back_end = start + count
-    return out_at, back_at, out_end
+    return out_at, back_at, out_end, back_end
 
 
 def route(idx_row, table, peers, n_exp, n_slot):
@@ -116,8 +115,7 @@
     seen = jnp.zeros((n_exp, lanes), f32)
     start_out = [jnp.zeros((n_exp, lanes), f32) for _ in range(MAX_COPIES)]
     start_back = [jnp.zeros((n_exp, lanes), f32) for _ in range(MAX_COPIES)]
-    total = jnp.zeros((1, lanes), f32)
-    stream_counts = []
+    stream_counts, over_out, over_back = [], [], []
     for r in range(len(peers)):
         seens, counts = [], []
         peer_hot = jnp.zeros((1, lanes), f32)
@@ -128,12 +126,13 @@
             counts.append(jnp.sum(here * (1.0 - own) * rows, axis=0, keepdims=True))
             peer_hot = peer_hot + s * jnp.sum(here * hot, axis=0, keepdims=True)
             seen = seen + here
-        out_at, back_at, end = stream_starts(counts, peer_hot)
+        out_at, back_at, out_end, back_end = stream_starts(counts, peer_hot)
         if r == 0:
             hot_slot = peer_hot
         if r >= 2:
             stream_counts.append(counts)
-            total = jnp.maximum(total, end)
+            over_out.append(jnp.maximum(out_end - DIRECT, 0.0))
+            over_back.append(jnp.maximum(back_end - DIRECT, 0.0))
         for s in range(n_slot):
             local = LOCAL_BASE + SLOT_ROWS * own_slot + SEG * r
             if r == 0:
@@ -142,8 +141,8 @@
                 seg = s - (peer_hot < s).astype(f32)
                 code_out = code_back = jnp.where(own > 0, local, STREAM_AT[1] + SEG * seg)
             else:
-                code_out = jnp.where(own > 0, local, STREAM_AT[r] + out_at[s])
-                code_back = jnp.where(own > 0, local, STREAM_AT[r] + back_at[s])
+                code_out = jnp.where(own > 0, local, RAW_AT[r] + out_at[s])
+                code_back = jnp.where(own > 0, local, RAW_AT[r] + back_at[s])
             for c in range(MAX_COPIES):
                 mine = (match[r][s] > 0) & (seens[s] == c)
                 start_out[c] = jnp.where(mine, code_out, start_out[c])
@@ -153,16 +152,25 @@
     row = jnp.floor((rank + 0.5) * wide(per_copy))
     which = rank - row * wide(copies)
     codes = []
-    for starts in (start_out, start_back):
+    for starts, over in ((start_out, over_out), (start_back, over_back)):
         start = wide(starts[3])
         for c in range(MAX_COPIES - 1):
             start = jnp.where(which == c, wide(starts[c]), start)
-        codes.append(jnp.sum(onehot * (start + row), axis=0, keepdims=True).astype(jnp.int32))
-    fits = jnp.max(own * hot, axis=0, keepdims=True) * (total <= PAIR).astype(f32)
-    return codes, hot_slot, stream_counts, fits
-
-
-def layer_kernel(slot_expert, topk_idx, topk_w, tokens, w_up, w_down, out, last_rows, last_mask, last_gate, found, table, idx_row, gate_row, tok_buf, up_buf, down_buf, send_core, recv_core, send_chip, recv_chip, acc, rows_buf, back_core, back_chip, early, mixed, mask_buf, gate_buf, code_row, back_row, code_col, gate_col, counts_out, counts_in, flags, t_sem, w_sem, ds_sem, dr_sem, bs_sem, br_sem, o_sem, cs_sem, cr_sem, fs_sem, fr_sem):
+        raw = jnp.sum(onehot * (start + row), axis=0, keepdims=True)
+        code = raw
+        for r, first in ((2, 0.0), (3, over[0][:, :1])):
+            at = raw - RAW_AT[r]
+            code = jnp.where(at >= 0, jnp.where(at < DIRECT, STREAM_AT[r] + at, SHARED_AT + first + (at - DIRECT)), code)
+        codes.append(code.astype(jnp.int32))
+    over = jnp.maximum(over_out[0] + over_out[1], over_back[0] + over_back[1])
+    fits = jnp.max(own * hot, axis=0, keepdims=True) * (over <= SHARED).astype(f32)
+    zero = jnp.zeros((1, lanes), f32)
+    tables = [jnp.concatenate(stream_counts[0] + [zero] * (8 - n_slot), axis=0),
+              jnp.concatenate(stream_counts[1] + [over_out[0], over_back[0]] + [zero] * (6 - n_slot), axis=0)]
+    return codes, hot_slot, tables, fits
+
+
+def layer_kernel(slot_expert, topk_idx, topk_w, tokens, w_up, w_down, out, last_rows, last_mask, last_gate, found, table, idx_row, gate_row, tok_buf, up_buf, down_buf, send_core, recv_core, send_chip, send_shared, recv_chip, acc, rows_buf, back_core, back_chip, back_shared, swap_out, swap_in, early, mixed, mask_buf, gate_buf, code_row, back_row, code_col, gate_col, counts_out, counts_in, flags, t_sem, w_sem, ds_sem, dr_sem, bs_sem, br_sem, o_sem, cs_sem, cr_sem, fs_sem, fr_sem, xs_sem, xr_sem):
     f32, bf16 = jnp.float32, jnp.bfloat16
     n_tok, d_model = tok_buf.shape
     n_slot = w_up.shape[0]
@@ -191,12 +199,12 @@
     token_copy.start()
     for copy in small_copies:
         copy.wait()
-    (code_out, code_back), hot_slot, stream_counts, fits = route(idx_row[...], table, peers, 16, n_slot)
+    (code_out, code_back), hot_slot, count_tables, fits = route(idx_row[...], table, peers, 16, n_slot)
     code_row[...] = jnp.broadcast_to(code_out, code_row.shape)
     back_row[...] = jnp.broadcast_to(code_back, back_row.shape)
     hot_slot = hot_slot[:, :1]
     for r in (2, 3):
-        counts_out[r - 2] = jnp.concatenate(stream_counts[r - 2] + [jnp.zeros((8 - n_slot, 128), f32)], axis=0)
+        counts_out[r - 2] = count_tables[r - 2]
     flags[0] = jnp.broadcast_to(fits, (8, 128))
 
     def pick(ids):
@@ -207,27 +215,44 @@
         return lax.broadcasted_iota(jnp.int32, (rows, n_tok), 0) + first
 
     def dispatch_copy(k, r):
+        to = r
         if r == 1:
             rows = pl.ds(k * SEG, SEG)
             src, dst = send_core.at[rows], recv_core.at[rows]
+        elif k < N_SEG - 1:
+            rows = pl.ds(SEND_AT[k], SEND_AT[k + 1] - SEND_AT[k])
+            src, dst = send_chip.at[r - 2, rows], recv_chip.at[r - 2, rows]
+        elif r == 2:
+            src, dst = send_shared, recv_chip.at[0, pl.ds(DIRECT, SHARED)]
         else:
-            rows = pl.ds(SEND_AT[k], chunk_rows(k)[0])
-            src, dst = send_chip.at[r - 2, rows], recv_chip.at[r - 2, rows]
+            to = 1
+            src, dst = recv_chip.at[0, pl.ds(DIRECT, SHARED)], recv_chip.at[1, pl.ds(DIRECT, SHARED)]
         return pltpu.make_async_remote_copy(
             src_ref=src, dst_ref=dst, send_sem=ds_sem.at[k, r - 1], recv_sem=dr_sem.at[k, r - 1],
-            device_id=peer_ids[r], device_id_type=MESH)
+            device_id=peer_ids[to], device_id_type=MESH)
 
     def back_copy(k, r):
-        size = chunk_rows(k)[1]
+        size = BACK_AT[k + 1] - BACK_AT[k]
         if r == 1:
             src, to_early, to_last = back_core.at[pl.ds(k * SEG, SEG)], pl.ds(k * SEG, SEG), pl.ds(0, SEG)
         else:
             src = back_chip.at[r - 2, pl.ds(BACK_AT[k], size)]
             to_early = pl.ds(3 * SEG + (r - 2) * BACK_AT[3] + BACK_AT[k], size)
-            to_last = pl.ds((r - 1) * SEG, SEG)
+            to_last = pl.ds(SEG + (r - 2) * size, size)
         return pltpu.make_async_remote_copy(
             src_ref=src, dst_ref=early.at[to_early] if k < N_SEG - 1 else last_rows.at[to_last],
             send_sem=bs_sem.at[k, r - 1], recv_sem=br_sem.at[k, r - 1],
+            device_id=peer_ids[r], device_id_type=MESH)
+
+    last_size = BACK_AT[N_SEG] - BACK_AT[N_SEG - 1]
+
+    def shared_copy(r):
+        if r == 1:
+            src, dst = swap_out, swap_in
+        else:
+            src, dst = back_shared, last_rows.at[pl.ds(SEG + 2 * last_size, SHARED)]
+        return pltpu.make_async_remote_copy(
+            src_ref=src, dst_ref=dst, send_sem=xs_sem.at[r - 1], recv_sem=xr_sem.at[r - 1],
             device_id=peer_ids[r], device_id_type=MESH)
 
     def counts_copy(r):
@@ -246,17 +271,21 @@
         for copy in weight_copies(s):
             copy.start()
     for k in range(N_SEG):
-        size = chunk_rows(k)[0]
-        ids = [ids_from(STREAM_AT[2] + SEND_AT[k], size), ids_from(STREAM_AT[3] + SEND_AT[k], size), ids_from(k * SEG, SEG)]
-        picked = pick(jnp.concatenate(ids, axis=0))
-        send_chip[0, SEND_AT[k]:SEND_AT[k + 1], :] = picked[:size]
-        send_chip[1, SEND_AT[k]:SEND_AT[k + 1], :] = picked[size:2 * size]
-        send_core[k * SEG:(k + 1) * SEG, :] = picked[2 * size:]
+        if k < N_SEG - 1:
+            size = SEND_AT[k + 1] - SEND_AT[k]
+            ids = [ids_from(STREAM_AT[2] + SEND_AT[k], size), ids_from(STREAM_AT[3] + SEND_AT[k], size), ids_from(k * SEG, SEG)]
+            picked = pick(jnp.concatenate(ids, axis=0))
+            send_chip[0, SEND_AT[k]:SEND_AT[k + 1], :] = picked[:size]
+            send_chip[1, SEND_AT[k]:SEND_AT[k + 1], :] = picked[size:2 * size]
+        else:
+            picked = pick(jnp.concatenate([ids_from(SHARED_AT, SHARED), ids_from(k * SEG, SEG)], axis=0))
+            send_shared[...] = picked[:SHARED]
+        send_core[k * SEG:(k + 1) * SEG, :] = picked[-SEG:]
         if k == 0:
             pl.semaphore_wait(barrier, 4)
             for r in (2, 3):
                 counts_copy(r).start()
-        for r in (2, 3, 1):
+        for r in (2, 3, 1) if k < N_SEG - 1 else (2, 1):
             dispatch_copy(k, r).start()
     flag_copy(4).start()
 
@@ -268,16 +297,19 @@
     early[n_early:, :] = jnp.zeros((EARLY_ROWS - n_early, d_model), bf16)
     rows_buf[n_slot * SLOT_ROWS:, :] = jnp.zeros((LOCAL_ROWS - n_slot * SLOT_ROWS, d_model), bf16)
 
-    def last_ids(i):
-        core_id = STREAM_AT[1] + 3 * SEG + i
-        chip_id = jnp.where(i < 2 * SEG, STREAM_AT[2] + BACK_AT[3] - SEG, STREAM_AT[3] + BACK_AT[3] - 2 * SEG) + i
-        return jnp.where(i < SEG, core_id, jnp.where(i < 3 * SEG, chip_id, -1))
-
-    def early_ids(i):
-        chip_id = jnp.where(i < 3 * SEG + BACK_AT[3], STREAM_AT[2] - 3 * SEG, STREAM_AT[3] - 3 * SEG - BACK_AT[3]) + i
-        return jnp.where(i < 3 * SEG, STREAM_AT[1] + i, jnp.where(i < n_early, chip_id, -1))
-
-    ids = last_ids(lax.broadcasted_iota(jnp.int32, (3 * SEG, n_tok), 0))
+    def piecewise(i, pieces):
+        ids, at = jnp.full_like(i, -1), sum(size for _, size in pieces)
+        for first, size in reversed(pieces):
+            ids = jnp.where(i < at, i + (first - at + size), ids)
+            at -= size
+        return ids
+
+    last_ids = lambda i: piecewise(i, [(STREAM_AT[1] + 3 * SEG, SEG), (STREAM_AT[2] + BACK_AT[3], last_size),
+                                       (STREAM_AT[3] + BACK_AT[3], last_size), (SHARED_AT, SHARED)])
+    early_ids = lambda i: piecewise(i, [(STREAM_AT[1], 3 * SEG), (STREAM_AT[2], BACK_AT[3]), (STREAM_AT[3], BACK_AT[3])])
+    n_last = SEG + 2 * last_size + SHARED
+
+    ids = last_ids(lax.broadcasted_iota(jnp.int32, (n_last, n_tok), 0))
     gates = jnp.sum(jnp.where(ids == back_row[0:1, :], gate_row[...], 0.0), axis=1, keepdims=True)
     gate_buf[...] = jnp.broadcast_to(gates, gate_buf.shape)
     lane = lax.broadcasted_iota(jnp.int32, (n_tok, 128), 1)
@@ -294,13 +326,27 @@
     for r in (2, 3):
         counts_copy(r).wait_recv()
     in_counts = [[counts_in[j, s:s + 1, :1] for s in range(n_slot)] for j in range(2)]
+    in_first = [[counts_in[j, n_slot + d:n_slot + d + 1, :1] for d in range(2)] for j in range(2)]
     in_starts = [stream_starts(counts, hot_slot) for counts in in_counts]
     as_int = lambda a: a.astype(jnp.int32)
+
+    def returned(r, first, size, slots, shift):
+        slots = list(slots)
+        i = lax.broadcasted_iota(jnp.int32, (size, SEG * len(slots)), 0)
+        j = lax.broadcasted_iota(jnp.int32, (size, SEG * len(slots)), 1)
+        mask = jnp.zeros(i.shape, f32)
+        for n, q in enumerate(slots):
+            row = j - n * SEG
+            at = row + as_int(in_starts[r - 2][1][q])
+            fit = (at + shift == i + first) & (at >= first) & (row >= 0) & (row < as_int(in_counts[r - 2][q]))
+            mask = jnp.where(fit, 1.0, mask)
+        done = jnp.concatenate([rows_buf[q * SLOT_ROWS + r * SEG:q * SLOT_ROWS + (r + 1) * SEG, :] for q in slots], axis=0)
+        return jnp.dot(mask.astype(bf16), done, preferred_element_type=f32).astype(bf16)
 
     for s in range(n_slot):
         lo, hi = s * SLOT_ROWS, (s + 1) * SLOT_ROWS
         if s < N_SEG:
-            for r in (1, 2, 3):
+            for r in (1, 2, 3) if s < N_SEG - 1 else (1, 3):
                 dispatch_copy(s, r).wait_recv()
         near = rows_buf[lo + SEG:lo + 2 * SEG, :].astype(f32)
         if s < N_SEG:
@@ -308,11 +354,14 @@
         if s > 0:
             near = near + recv_core[(s - 1) * SEG:s * SEG, :].astype(f32) * (hot_slot < s).astype(f32)
         rows_buf[lo + SEG:lo + 2 * SEG, :] = near.astype(bf16)
-        come = SEND_AT[min(s, N_SEG - 1) + 1]
+        come = SEND_AT[s + 1] if s < N_SEG - 1 else DIRECT + SHARED
         i = lax.broadcasted_iota(jnp.int32, (SEG, come), 0)
         j = lax.broadcasted_iota(jnp.int32, (SEG, come), 1)
         for r in (2, 3):
-            mask = (j - i == as_int(in_starts[r - 2][0][s])) & (i < as_int(in_counts[r - 2][s]))
+            at = i + as_int(in_starts[r - 2][0][s])
+            if s >= N_SEG - 1:
+                at = jnp.where(at < DIRECT, at, at + as_int(in_first[r - 2][0]))
+            mask = (j == at) & (i < as_int(in_counts[r - 2][s]))
             far = jnp.dot(mask.astype(f32).astype(bf16), recv_chip[r - 2, :come, :], preferred_element_type=f32)
             at = slice(lo + r * SEG, lo + (r + 1) * SEG)
             rows_buf[at, :] = (rows_buf[at, :].astype(f32) + far).astype(bf16)
@@ -333,26 +382,27 @@
             for copy in weight_copies(s + N_WBUF):
                 copy.start()
         rows_buf[lo:hi, :] = acc[...].astype(bf16)
+        if s == N_SEG - 2:
+            dispatch_copy(N_SEG - 1, 2).wait_recv()
+            dispatch_copy(N_SEG - 1, 3).start()
         if s > 0:
             k = s - 1
-            size = chunk_rows(k)[1]
-            slots = list(range(max(k - 1, 0), s + 1))
-            i = lax.broadcasted_iota(jnp.int32, (size, SEG * len(slots)), 0)
-            j = lax.broadcasted_iota(jnp.int32, (size, SEG * len(slots)), 1)
+            if k == N_SEG - 1:
+                swap_out[...] = returned(3, DIRECT, SHARED, (s - 1, s), as_int(in_first[1][1]))
+                shared_copy(1).start()
             for r in (2, 3):
-                mask = jnp.zeros(i.shape, f32)
-                for n, q in enumerate(slots):
-                    row = j - n * SEG
-                    fit = (i + BACK_AT[k] - row == as_int(in_starts[r - 2][1][q])) & (row >= 0) & (row < as_int(in_counts[r - 2][q]))
-                    mask = jnp.where(fit, 1.0, mask)
-                done = jnp.concatenate([rows_buf[q * SLOT_ROWS + r * SEG:q * SLOT_ROWS + (r + 1) * SEG, :] for q in slots], axis=0)
-                back_chip[r - 2, BACK_AT[k]:BACK_AT[k + 1], :] = jnp.dot(mask.astype(bf16), done, preferred_element_type=f32).astype(bf16)
+                back_chip[r - 2, BACK_AT[k]:BACK_AT[k + 1], :] = returned(r, BACK_AT[k], BACK_AT[k + 1] - BACK_AT[k], range(max(k - 2, 0), s + 1), 0)
                 back_copy(k, r).start()
             prev = rows_buf[lo - SLOT_ROWS + SEG:lo - SLOT_ROWS + 2 * SEG, :].astype(f32)
             last = rows_buf[lo + SEG:lo + 2 * SEG, :].astype(f32)
             back = prev * (hot_slot > k).astype(f32) + last * (hot_slot <= k).astype(f32)
             back_core[k * SEG:(k + 1) * SEG, :] = back.astype(bf16)
             back_copy(k, 1).start()
+            if k == N_SEG - 1:
+                mine = returned(2, DIRECT, SHARED, (s - 1, s), as_int(in_first[0][1]))
+                shared_copy(1).wait_recv()
+                back_shared[...] = (mine.astype(f32) + swap_in[...].astype(f32)).astype(bf16)
+                shared_copy(2).start()
 
     tile = 256
     n_tile = n_tok // tile
@@ -385,6 +435,8 @@
     for k in range(N_SEG):
         for r in (1, 2, 3):
             back_copy(k, r).wait_recv()
+        if k == N_SEG - 1:
+            shared_copy(2).wait_recv()
         if k == N_SEG - 2:
             combine(early_ids, EARLY_ROWS, early, True)
             for i in range(n_tile):
@@ -393,6 +445,8 @@
                 copy.wait()
     for r in (2, 3):
         counts_copy(r).wait_send()
+    for r in (1, 2):
+        shared_copy(r).wait_send()
     for r in (1, 2, 3, 4):
         flag_copy(r).wait_send()
     for k in range(N_SEG):
@@ -448,12 +502,16 @@
             pltpu.VMEM((N_WBUF, d_ff, d_model), bf16),
             pltpu.VMEM((N_SEG * SEG, d_model), bf16),
             pltpu.VMEM((N_SEG * SEG, d_model), bf16),
-            pltpu.VMEM((2, PAIR, d_model), bf16),
-            pltpu.VMEM((2, PAIR, d_model), bf16),
+            pltpu.VMEM((2, DIRECT, d_model), bf16),
+            pltpu.VMEM((SHARED, d_model), bf16),
+            pltpu.VMEM((2, DIRECT + SHARED, d_model), bf16),
             pltpu.VMEM((SLOT_ROWS, d_model), f32),
             pltpu.VMEM((LOCAL_ROWS, d_model), bf16),
             pltpu.VMEM((N_SEG * SEG, d_model), bf16),
-            pltpu.VMEM((2, PAIR, d_model), bf16),
+            pltpu.VMEM((2, DIRECT, d_model), bf16),
+            pltpu.VMEM((SHARED, d_model), bf16),
+            pltpu.VMEM((SHARED, d_model), bf16),
+            pltpu.VMEM((SHARED, d_model), bf16),
             pltpu.VMEM((EARLY_ROWS, d_model), bf16),
             pltpu.VMEM((n_tok, d_model), bf16),
             pltpu.VMEM((n_tok, LAST_ROWS), bf16),
@@ -467,7 +525,7 @@
             pltpu.VMEM((6, 8, 128), f32),
             dma((6,)), dma((n_slot, 2)),
             dma((N_SEG, 3)), dma((N_SEG, 3)), dma((N_SEG, 3)), dma((N_SEG, 3)),
-            dma((n_tok // 256,)), dma((2,)), dma((2,)), dma((4,)), dma((4,)),
+            dma((n_tok // 256,)), dma((2,)), dma((2,)), dma((4,)), dma((4,)), dma((2,)), dma((2,)),
         ],
         compiler_params=pltpu.CompilerParams(collective_id=0, has_side_effects=True, vmem_limit_bytes=60 * 1024 * 1024),
     )(slot_expert, topk_idx.reshape(1, n_tok), topk_w.reshape(1, n_tok), tokens, w_up[0], w_down[0])

time: 49.2 us -> 50.3 us (1.022)
  Pallas kernels: 47.2 us -> 48.2 us
    pallas_call x1, Pallas kernels: 45.3 us -> 46.3 us  [fast_layer(): pl.pallas_call(layer_kernel, out_shape=(shape((n_tok, d_model), bf16), sh...]
where the time goes in v6:
time: 50.3 us; the launch traced here: 50.2 us
  Pallas kernels  48.2 us (96%)
  local copies, waits for them, and re-layouts  1.15 us (2%)
  between operations  0.75 us (1%)
    pallas_call x1, Pallas kernels, fast_layer(): pl.pallas_call(layer_kernel, out_shape=(shape((n_tok, d_model), bf16), sh...  46.3 us
    pallas_call x1, Pallas kernels, add_last(): pl.pallas_call(last_kernel, grid=(n_tok // tile,), out_shape=jax.ShapeDty...  1.94 us
    unnamed x10, local copies, waits for them, and re-layouts  1.15 us

profile of v6, /device:TPU:0, one launch (start us, length us, event | category | flops | bytes accessed | tf_op | source)
XLA Modules:
  0.0 50.2 jit_solution(1677258801147429722)
XLA Ops:
  0.0 0.0 copy-start
  0.0 0.0 copy-start.2
  0.0 0.0 copy-start.3
  0.0 0.0 copy-start.4
  0.0 46.3 %shard_map.66 = (bf16[1024,768]{1,0:T(8,128)(2,1)}, bf16[240,768]{1,0:T(8,128)(2,1)S(1)}, bf16[1024,256]{1,0:T(8,128)(2,1)S(1)}, f32[240,128]{1,0:T(8,128)S(1)}, s32[1,128]{1,0:T(1,128)}) custom-call(s32[4,5]{1,0:T(4,128)} %slot_expert.1, s32[1,1024]{1,0:T(1,128)} %bitcast.76, f32[1,1024]{1,0:T(1,128)} %bitcast.83, bf16[1024,768]{1,0:T(8,128)(2,1)} %tokens.1, ...), custom_call_target="tpu_custom_call" | custom-call | tf_op jit(solution)/shard_map/pallas_call | solution.py:490
  47.0 0.0 copy-done
  47.0 0.0 copy-done.2
  47.0 0.0 copy-done.3
  47.0 0.0 copy-done.4
  47.0 2.0 %conditional.1 = (bf16[1024,768]{1,0:T(8,128)(2,1)S(1)}) conditional(s32[]{:T(128)} %bitcast.40, (s32[4,5]{1,0:T(4,128)S(1)}, s32[1024,1]{0,1:T(1,128)S(1)}, bf16[1024,768]{1,0:T(8,128)(2,1)S(1)}, bf16[1,5,768,3072]{3,2,1,0:T(8,128)(2,1)}, bf16[1,5,3072,768]{3,2,1,0:T(8,128)(2,1)}, /*index=5*/f32[1024,1]{0,1:T(1,128)S(1)}) %tuple.46, ...), branch_computations={%region_0.8_spmd, %region_8.9_spmd} | conditional | flops 14581685248 | bytes 137039296 | solution.py:538
  47.1 1.9 %branch_1_fun.1 = bf16[1024,768]{1,0:T(8,128)(2,1)S(1)} custom-call(bf16[1024,768]{1,0:T(8,128)(2,1)} %get-tuple-element.34.part, bf16[240,768]{1,0:T(8,128)(2,1)S(1)} %get-tuple-element.35.rows, bf16[1024,256]{1,0:T(8,128)(2,1)S(1)} %get-tuple-element.36.mask, f32[240,128]{1,0:T(8,128)S(1)} %get-tuple-element.37.gate), custom_call_target="tpu_custom_call" | custom-call | tf_op jit(solution)/shard_map/cond/branch_1_fun/pallas_call | solution.py:473
  49.0 0.0 copy-start.1
  49.0 1.1 %copy-done.1 = bf16[1024,768]{1,0:T(8,128)(2,1)} copy-done((bf16[1024,768]{1,0:T(8,128)(2,1)}, bf16[1024,768]{1,0:T(8,128)(2,1)S(1)}, u32[]{:S(2)}) %copy-start.1) | copy-done | bytes 1572888
Async XLA Ops:
  0.0 47.0 %copy-start = (bf16[1024,768]{1,0:T(8,128)(2,1)S(1)}, bf16[1024,768]{1,0:T(8,128)(2,1)}, u32[]{:S(2)}) copy-start(bf16[1024,768]{1,0:T(8,128)(2,1)} %tokens.1) | copy-start | bytes 4718596
  0.0 47.0 %copy-start.2 = (s32[1024,1]{0,1:T(1,128)S(1)}, s32[1024,1]{0,1:T(1,128)}, u32[]{:S(2)}) copy-start(s32[1024,1]{0,1:T(1,128)} %param.9) | copy-start | bytes 12292
  0.0 47.0 %copy-start.3 = (s32[4,5]{1,0:T(4,128)S(1)}, s32[4,5]{1,0:T(4,128)}, u32[]{:S(2)}) copy-start(s32[4,5]{1,0:T(4,128)} %slot_expert.1) | copy-start | bytes 244
  0.0 47.0 %copy-start.4 = (f32[1024,1]{0,1:T(1,128)S(1)}, f32[1024,1]{0,1:T(1,128)}, u32[]{:S(2)}) copy-start(f32[1024,1]{0,1:T(1,128)} %param.10) | copy-start | bytes 12292
  49.0 1.1 %copy-start.1 = (bf16[1024,768]{1,0:T(8,128)(2,1)}, bf16[1024,768]{1,0:T(8,128)(2,1)S(1)}, u32[]{:S(2)}) copy-start(bf16[1024,768]{1,0:T(8,128)(2,1)S(1)} %get-tuple-element.83) | copy-start | bytes 4718596

commit v7 on v6

--- a/solution.py
+++ b/solution.py
@@ -343,17 +343,48 @@
         done = jnp.concatenate([rows_buf[q * SLOT_ROWS + r * SEG:q * SLOT_ROWS + (r + 1) * SEG, :] for q in slots], axis=0)
         return jnp.dot(mask.astype(bf16), done, preferred_element_type=f32).astype(bf16)
 
-    for s in range(n_slot):
-        lo, hi = s * SLOT_ROWS, (s + 1) * SLOT_ROWS
+    half = SLOT_ROWS // 2
+
+    def experts(s, first, size, width):
+        b = s % N_WBUF
+        rows = pl.ds(pl.multiple_of(s * SLOT_ROWS + first, half), size)
+
+        def ff_step(i, carry):
+            cols = pl.ds(pl.multiple_of(i * width, width), width)
+            pre = jnp.dot(rows_buf[rows, :], up_buf[b, :, cols], preferred_element_type=f32)
+            hidden = jax.nn.gelu(pre, approximate=True).astype(bf16)
+            acc[:size, :] += jnp.dot(hidden, down_buf[b, cols, :], preferred_element_type=f32)
+            return carry
+
+        acc[:size, :] = jnp.zeros((size, d_model), f32)
+        lax.fori_loop(0, d_ff // width, ff_step, 0)
+        rows_buf[rows, :] = acc[:size, :].astype(bf16)
+
+    def near_in(s):
+        lo = s * SLOT_ROWS + SEG
         if s < N_SEG:
-            for r in (1, 2, 3) if s < N_SEG - 1 else (1, 3):
+            dispatch_copy(s, 1).wait_recv()
+        mixed_in = rows_buf[lo:lo + SEG, :].astype(f32)
+        if s < N_SEG:
+            mixed_in = mixed_in + recv_core[s * SEG:(s + 1) * SEG, :].astype(f32) * (hot_slot > s).astype(f32)
+        if s > 0:
+            mixed_in = mixed_in + recv_core[(s - 1) * SEG:s * SEG, :].astype(f32) * (hot_slot < s).astype(f32)
+        rows_buf[lo:lo + SEG, :] = mixed_in.astype(bf16)
+
+    def near_out(s):
+        lo = s * SLOT_ROWS + SEG
+        if s > 0:
+            k = s - 1
+            prev = rows_buf[lo - SLOT_ROWS:lo - SLOT_ROWS + SEG, :].astype(f32)
+            last = rows_buf[lo:lo + SEG, :].astype(f32)
+            back = prev * (hot_slot > k).astype(f32) + last * (hot_slot <= k).astype(f32)
+            back_core[k * SEG:(k + 1) * SEG, :] = back.astype(bf16)
+            back_copy(k, 1).start()
+
+    def far_in(s):
+        if s < N_SEG:
+            for r in (2, 3) if s < N_SEG - 1 else (3,):
                 dispatch_copy(s, r).wait_recv()
-        near = rows_buf[lo + SEG:lo + 2 * SEG, :].astype(f32)
-        if s < N_SEG:
-            near = near + recv_core[s * SEG:(s + 1) * SEG, :].astype(f32) * (hot_slot > s).astype(f32)
-        if s > 0:
-            near = near + recv_core[(s - 1) * SEG:s * SEG, :].astype(f32) * (hot_slot < s).astype(f32)
-        rows_buf[lo + SEG:lo + 2 * SEG, :] = near.astype(bf16)
         come = SEND_AT[s + 1] if s < N_SEG - 1 else DIRECT + SHARED
         i = lax.broadcasted_iota(jnp.int32, (SEG, come), 0)
         j = lax.broadcasted_iota(jnp.int32, (SEG, come), 1)
@@ -362,29 +393,11 @@
             if s >= N_SEG - 1:
                 at = jnp.where(at < DIRECT, at, at + as_int(in_first[r - 2][0]))
             mask = (j == at) & (i < as_int(in_counts[r - 2][s]))
-            far = jnp.dot(mask.astype(f32).astype(bf16), recv_chip[r - 2, :come, :], preferred_element_type=f32)
-            at = slice(lo + r * SEG, lo + (r + 1) * SEG)
-            rows_buf[at, :] = (rows_buf[at, :].astype(f32) + far).astype(bf16)
-        for copy in weight_copies(s):
-            copy.wait()
-        b = s % N_WBUF
-        acc[...] = jnp.zeros_like(acc)
-
-        def ff_step(i, carry):
-            cols = pl.ds(pl.multiple_of(i * FF_TILE, FF_TILE), FF_TILE)
-            pre = jnp.dot(rows_buf[lo:hi, :], up_buf[b, :, cols], preferred_element_type=f32)
-            hidden = jax.nn.gelu(pre, approximate=True).astype(bf16)
-            acc[...] += jnp.dot(hidden, down_buf[b, cols, :], preferred_element_type=f32)
-            return carry
-
-        lax.fori_loop(0, d_ff // FF_TILE, ff_step, 0)
-        if s + N_WBUF < n_slot:
-            for copy in weight_copies(s + N_WBUF):
-                copy.start()
-        rows_buf[lo:hi, :] = acc[...].astype(bf16)
-        if s == N_SEG - 2:
-            dispatch_copy(N_SEG - 1, 2).wait_recv()
-            dispatch_copy(N_SEG - 1, 3).start()
+            came = jnp.dot(mask.astype(f32).astype(bf16), recv_chip[r - 2, :come, :], preferred_element_type=f32)
+            rows = slice(s * SLOT_ROWS + r * SEG, s * SLOT_ROWS + (r + 1) * SEG)
+            rows_buf[rows, :] = (rows_buf[rows, :].astype(f32) + came).astype(bf16)
+
+    def far_out(s):
         if s > 0:
             k = s - 1
             if k == N_SEG - 1:
@@ -393,17 +406,46 @@
             for r in (2, 3):
                 back_chip[r - 2, BACK_AT[k]:BACK_AT[k + 1], :] = returned(r, BACK_AT[k], BACK_AT[k + 1] - BACK_AT[k], range(max(k - 2, 0), s + 1), 0)
                 back_copy(k, r).start()
-            prev = rows_buf[lo - SLOT_ROWS + SEG:lo - SLOT_ROWS + 2 * SEG, :].astype(f32)
-            last = rows_buf[lo + SEG:lo + 2 * SEG, :].astype(f32)
-            back = prev * (hot_slot > k).astype(f32) + last * (hot_slot <= k).astype(f32)
-            back_core[k * SEG:(k + 1) * SEG, :] = back.astype(bf16)
-            back_copy(k, 1).start()
             if k == N_SEG - 1:
                 mine = returned(2, DIRECT, SHARED, (s - 1, s), as_int(in_first[0][1]))
                 shared_copy(1).wait_recv()
                 back_shared[...] = (mine.astype(f32) + swap_in[...].astype(f32)).astype(bf16)
                 shared_copy(2).start()
 
+    def weights_in(s):
+        for copy in weight_copies(s):
+            copy.wait()
+
+    def prepare(s):
+        near_in(s)
+        far_in(s)
+        weights_in(s)
+
+    def finish(s):
+        if s == N_SEG - 2:
+            dispatch_copy(N_SEG - 1, 2).wait_recv()
+            dispatch_copy(N_SEG - 1, 3).start()
+        far_out(s)
+        near_out(s)
+
+    near_in(0)
+    weights_in(0)
+    experts(0, 0, half, FF_TILE)
+    far_in(0)
+    experts(0, half, half, FF_TILE)
+    for copy in weight_copies(N_WBUF):
+        copy.start()
+    inner = range(1, n_slot)
+
+    def step(t, carry):
+        for q in inner:
+            pl.when(t == q)(functools.partial(prepare, q))
+        experts(t, 0, SLOT_ROWS, d_ff)
+        for q in inner:
+            pl.when(t == q)(functools.partial(finish, q))
+        return carry
+
+    lax.fori_loop(1, n_slot, step, 0)
     tile = 256
     n_tile = n_tok // tile
 

time: 50.3 us -> 48.6 us (0.966)
  Pallas kernels: 48.2 us -> 46.6 us
    pallas_call x1, Pallas kernels: 46.3 us -> 44.6 us  [fast_layer(): pl.pallas_call(layer_kernel, out_shape=(shape((n_tok, d_model), bf16), sh...]
where the time goes in v7:
time: 48.6 us; the launch traced here: 48.5 us
  Pallas kernels  46.6 us (96%)
  local copies, waits for them, and re-layouts  1.15 us (2%)
  between operations  0.75 us (2%)
    pallas_call x1, Pallas kernels, fast_layer(): pl.pallas_call(layer_kernel, out_shape=(shape((n_tok, d_model), bf16), sh...  44.6 us
    pallas_call x1, Pallas kernels, add_last(): pl.pallas_call(last_kernel, grid=(n_tok // tile,), out_shape=jax.ShapeDty...  1.94 us
    unnamed x10, local copies, waits for them, and re-layouts  1.15 us

profile of v7, /device:TPU:0, one launch (start us, length us, event | category | flops | bytes accessed | tf_op | source)
XLA Modules:
  0.0 48.5 jit_solution(1754849361541805596)
XLA Ops:
  0.0 0.0 copy-start
  0.0 0.0 copy-start.2
  0.0 0.0 copy-start.3
  0.0 0.0 copy-start.4
  0.0 44.6 %shard_map.66 = (bf16[1024,768]{1,0:T(8,128)(2,1)}, bf16[240,768]{1,0:T(8,128)(2,1)S(1)}, bf16[1024,256]{1,0:T(8,128)(2,1)S(1)}, f32[240,128]{1,0:T(8,128)S(1)}, s32[1,128]{1,0:T(1,128)}) custom-call(s32[4,5]{1,0:T(4,128)} %slot_expert.1, s32[1,1024]{1,0:T(1,128)} %bitcast.76, f32[1,1024]{1,0:T(1,128)} %bitcast.83, bf16[1024,768]{1,0:T(8,128)(2,1)} %tokens.1, ...), custom_call_target="tpu_custom_call" | custom-call | tf_op jit(solution)/shard_map/pallas_call | solution.py:532
  45.4 0.0 copy-done
  45.4 0.0 copy-done.2
  45.4 0.0 copy-done.3
  45.4 0.0 copy-done.4
  45.4 2.0 %conditional.1 = (bf16[1024,768]{1,0:T(8,128)(2,1)S(1)}) conditional(s32[]{:T(128)} %bitcast.40, (s32[4,5]{1,0:T(4,128)S(1)}, s32[1024,1]{0,1:T(1,128)S(1)}, bf16[1024,768]{1,0:T(8,128)(2,1)S(1)}, bf16[1,5,768,3072]{3,2,1,0:T(8,128)(2,1)}, bf16[1,5,3072,768]{3,2,1,0:T(8,128)(2,1)}, /*index=5*/f32[1024,1]{0,1:T(1,128)S(1)}) %tuple.46, ...), branch_computations={%region_0.8_spmd, %region_8.9_spmd} | conditional | flops 14581685248 | bytes 137039296 | solution.py:580
  45.4 1.9 %branch_1_fun.1 = bf16[1024,768]{1,0:T(8,128)(2,1)S(1)} custom-call(bf16[1024,768]{1,0:T(8,128)(2,1)} %get-tuple-element.34.part, bf16[240,768]{1,0:T(8,128)(2,1)S(1)} %get-tuple-element.35.rows, bf16[1024,256]{1,0:T(8,128)(2,1)S(1)} %get-tuple-element.36.mask, f32[240,128]{1,0:T(8,128)S(1)} %get-tuple-element.37.gate), custom_call_target="tpu_custom_call" | custom-call | tf_op jit(solution)/shard_map/cond/branch_1_fun/pallas_call | solution.py:515
  47.4 0.0 copy-start.1
  47.4 1.1 %copy-done.1 = bf16[1024,768]{1,0:T(8,128)(2,1)} copy-done((bf16[1024,768]{1,0:T(8,128)(2,1)}, bf16[1024,768]{1,0:T(8,128)(2,1)S(1)}, u32[]{:S(2)}) %copy-start.1) | copy-done | bytes 1572888
Async XLA Ops:
  0.0 45.4 %copy-start = (bf16[1024,768]{1,0:T(8,128)(2,1)S(1)}, bf16[1024,768]{1,0:T(8,128)(2,1)}, u32[]{:S(2)}) copy-start(bf16[1024,768]{1,0:T(8,128)(2,1)} %tokens.1) | copy-start | bytes 4718596
  0.0 45.4 %copy-start.2 = (s32[1024,1]{0,1:T(1,128)S(1)}, s32[1024,1]{0,1:T(1,128)}, u32[]{:S(2)}) copy-start(s32[1024,1]{0,1:T(1,128)} %param.9) | copy-start | bytes 12292
  0.0 45.4 %copy-start.3 = (s32[4,5]{1,0:T(4,128)S(1)}, s32[4,5]{1,0:T(4,128)}, u32[]{:S(2)}) copy-start(s32[4,5]{1,0:T(4,128)} %slot_expert.1) | copy-start | bytes 244
  0.0 45.4 %copy-start.4 = (f32[1024,1]{0,1:T(1,128)S(1)}, f32[1024,1]{0,1:T(1,128)}, u32[]{:S(2)}) copy-start(f32[1024,1]{0,1:T(1,128)} %param.10) | copy-start | bytes 12292
  47.4 1.1 %copy-start.1 = (bf16[1024,768]{1,0:T(8,128)(2,1)}, bf16[1024,768]{1,0:T(8,128)(2,1)S(1)}, u32[]{:S(2)}) copy-start(bf16[1024,768]{1,0:T(8,128)(2,1)S(1)} %get-tuple-element.83) | copy-start | bytes 4718596
